TPU v7x, 32 devices: a whole 2x2x4 slice. The times are simulated.
32 devices in a mesh: pb: 2 (over x), col: 16 (over z, y, core).
Axes of the slice: x: 2, y: 2, z: 4, core: 2. Of those that a mesh axis runs over, the one named last changes fastest.
Arguments:
- queries: bfloat16 [4096, 1024], P(('pb', 'col')), may hold values from -64 to 64
- candidates: bfloat16 [16384, 1024], P(('col', 'pb')), may hold values from -5 to 5
- grades: int32 [4096, 16384], P('pb', 'col'), may hold values from 0 to 4
- query_weights: float32 [4096], P('pb'), may hold values from -0.046875 to 0.046875
Outputs:
- losses: float32 [4096], P('pb')
- query_grad: bfloat16 [4096, 1024], P(('pb', 'col'))
- cand_grad: bfloat16 [16384, 1024], P(('col', 'pb'))
All inputs are finite; a program needn't handle non-finite values.
Results may differ from a plain program's by a relative error of at most 0.0071.
Values may be sent and summed in bfloat16 or wider, within the bound.
A program may use at most 128 MiB of HBM per device.

v0:
```python
import functools
import math

import jax
import jax.numpy as jnp
from jax import lax
from jax.experimental import pallas as pl
from jax.experimental.pallas import tpu as pltpu
from jax.sharding import PartitionSpec as P

GRADES = 5
STATS = 16
LOWEST = -1e30
MESH = pl.DeviceIdType.MESH
F32 = jnp.float32
BF16 = jnp.bfloat16


def dev(p, i):
    return {"pb": p, "col": i}


class Place:
    def __init__(self, n_col, n_pb):
        self.n_col, self.n_pb = n_col, n_pb
        self.cores = 2 if n_col % 2 == 0 else 1
        rest = n_col // self.cores
        self.mids = 2 if rest % 2 == 0 else 1
        self.outs = rest // self.mids
        self.me = lax.axis_index("col")
        self.p = lax.axis_index("pb")
        self.core = lax.rem(self.me, self.cores)
        chip = self.me // self.cores
        self.mid = lax.rem(chip, self.mids)
        self.out = chip // self.mids

    def index(self, do, dm, dc):
        o = lax.rem(self.out + do, self.outs)
        m = lax.rem(self.mid + dm, self.mids)
        c = lax.rem(self.core + dc, self.cores)
        return (o * self.mids + m) * self.cores + c

    def peers(self):
        found = [dev(self.p, self.index(d, 0, 0)) for d in range(1, self.outs)]
        found += [dev(self.p, self.index(0, d, 0)) for d in range(1, self.mids)]
        found += [dev(self.p, self.index(0, 0, d)) for d in range(1, self.cores)]
        found += [dev(lax.rem(self.p + d, self.n_pb), self.me) for d in range(1, self.n_pb)]
        return found


def greet(peers):
    barrier = pltpu.get_barrier_semaphore()
    for peer in peers:
        pl.semaphore_signal(barrier, inc=1, device_id=peer, device_id_type=MESH)
    pl.semaphore_wait(barrier, len(peers))


def remote(src, dst, send, recv, device):
    return pltpu.make_async_remote_copy(
        src_ref=src, dst_ref=dst, send_sem=send, recv_sem=recv, device_id=device, device_id_type=MESH
    )


def score_tile(scaling, q, c, grades):
    rows = grades.shape[0]
    scores = lax.dot_general(q, c, (((1,), (1,)), ((), ())), preferred_element_type=F32) * scaling
    lane = lax.broadcasted_iota(jnp.int32, (rows, rows), 1)
    table = jnp.zeros((rows, rows), F32)
    picked = jnp.zeros(scores.shape, F32)
    for b in range(GRADES):
        member = grades == b
        highest = jnp.max(jnp.where(member, scores, LOWEST), axis=1, keepdims=True)
        picked = jnp.where(member, highest, picked)
        table = jnp.where(lane == b, highest, table)
    expo = jnp.exp(scores - picked)
    for b in range(GRADES):
        member = grades == b
        mass = jnp.sum(jnp.where(member, expo, 0.0), axis=1, keepdims=True)
        table = jnp.where(lane == GRADES + b, mass, table)
    assert scores.shape[1] < 4096
    rest = jnp.full((rows, 1), float(scores.shape[1]), F32)
    for b in range(0, GRADES - 1, 2):
        pair = jnp.where(grades == b, 1.0, jnp.where(grades == b + 1, 4096.0, 0.0))
        pair = jnp.sum(pair, axis=1, keepdims=True)
        high = jnp.floor(pair * (1.0 / 4096.0))
        low = pair - high * 4096.0
        table = jnp.where(lane == 2 * GRADES + b, low, table)
        table = jnp.where(lane == 2 * GRADES + b + 1, high, table)
        rest = rest - low - high
    table = jnp.where(lane == 3 * GRADES - 1, rest, table)
    total = jnp.sum(scores, axis=1, keepdims=True)
    table = jnp.where(lane == 3 * GRADES, total, table)
    return expo, table.T[:STATS]


def front_kernel(
    n_col, n_pb, scaling, q_ref, c_ref, g_hbm, q_all, c_all, e_hbm, s_all,
    g_all, e_all, q_send, q_recv, c_send, c_recv, own_sem, e_sem,
):
    at = Place(n_col, n_pb)
    rows, half = q_ref.shape[0], c_ref.shape[0]
    grades_in = pltpu.make_async_copy(g_hbm, g_all, own_sem.at[0])
    grades_in.start()
    own = [
        pltpu.make_async_copy(q_ref, q_all.at[at.me], own_sem.at[1]),
        pltpu.make_async_copy(c_ref, c_all.at[at.p], own_sem.at[2]),
    ]
    for copy in own:
        copy.start()
    greet(at.peers())
    c_copies = []
    for d in range(1, n_pb):
        other = lax.rem(at.p + d, n_pb)
        copy = remote(c_ref, c_all.at[at.p], c_send.at[d], c_recv.at[at.p], dev(other, at.me))
        copy.start()
        c_copies.append(copy)
    sends = []

    def push(src, block, device):
        copy = remote(src, q_all.at[block], q_send.at[len(sends)], q_recv.at[block], device)
        copy.start()
        sends.append(copy)

    def arrived(block):
        remote(q_ref, q_all.at[block], q_send.at[0], q_recv.at[block], dev(at.p, at.me)).wait_recv()

    def forward(do, dm):
        block = at.index(do, dm, 0)
        src = q_ref
        if do or dm:
            arrived(block)
            src = q_all.at[block]
        if dm == 0:
            if do == 0:
                for d in order[1:]:
                    push(src, block, dev(at.p, at.index(d, 0, 0)))
            for d in range(1, at.mids):
                push(src, block, dev(at.p, at.index(0, d, 0)))
        for d in range(1, at.cores):
            push(src, block, dev(at.p, at.index(0, 0, d)))

    def task(block, part):
        span = pl.ds(pl.multiple_of(block * rows, rows), rows)
        columns = pl.ds(pl.multiple_of(part * half, half), half)
        expo, stats = score_tile(scaling, q_all[block], c_all[part], g_all[span, columns])
        e_all[block, part] = expo
        s_all[block, part] = stats
        pltpu.make_async_copy(
            e_all.at[block, part], e_hbm.at[block, part], e_sem.at[block, part]
        ).start()

    order = [0] + sorted(range(1, at.outs), key=lambda d: min(d, at.outs - d))
    last = order[-1]

    def group(pairs):
        first = pairs[0]
        step = [b - a for a, b in zip(first, pairs[-1])]

        def body(j, carry):
            which = j // at.cores
            dc = lax.rem(j, at.cores)
            block = at.index(first[0] + which * step[0], first[1] + which * step[1], dc)

            @pl.when(dc > 0)
            def _():
                arrived(block)

            task(block, at.p)
            return carry

        lax.fori_loop(0, len(pairs) * at.cores, body, 0)

    for k in range(at.outs):
        pairs = [(order[k], 0)]
        if k > 0 and at.mids > 1:
            pairs.append((order[k - 1], 1))
        for pair in pairs:
            forward(*pair)
        if k == 0:
            for copy in own:
                copy.wait()
            grades_in.wait()
        group(pairs)

    def later(first, count):
        for d in range(1, n_pb):
            part = lax.rem(at.p + d, n_pb)

            def body(j, carry):
                do = last + 1 + j // (at.mids * at.cores)
                dm = lax.rem(j // at.cores, at.mids)
                task(at.index(do, dm, lax.rem(j, at.cores)), part)
                return carry

            if first == 0:
                remote(
                    c_ref, c_all.at[part], c_send.at[0], c_recv.at[part], dev(at.p, at.me)
                ).wait_recv()
            lax.fori_loop(first, first + count, body, 0)

    tail = at.cores if at.mids > 1 else 0
    if tail:
        forward(last, 1)
    later(0, n_col - tail)
    if tail:
        group([(last, 1)])
        later(n_col - tail, tail)

    def drain(j, carry):
        for part in range(n_pb):
            pltpu.make_async_copy(e_all.at[j, part], e_hbm.at[j, part], e_sem.at[j, part]).wait()
        return carry

    lax.fori_loop(0, n_col, drain, 0)
    for copy in sends + c_copies:
        copy.wait_send()


def front(q, c, grades, n_col, n_pb, scaling):
    vmem = pl.BlockSpec(memory_space=pltpu.VMEM)
    hbm = pl.BlockSpec(memory_space=pl.ANY)
    rows, half = q.shape[0], c.shape[0]
    e_shape = (n_col, n_pb, rows, half)
    dma = pltpu.SemaphoreType.DMA
    return pl.pallas_call(
        functools.partial(front_kernel, n_col, n_pb, scaling),
        out_shape=(
            jax.ShapeDtypeStruct((n_col, *q.shape), q.dtype),
            jax.ShapeDtypeStruct((n_pb, *c.shape), c.dtype),
            jax.ShapeDtypeStruct(e_shape, F32),
            jax.ShapeDtypeStruct((n_col, n_pb, STATS, rows), F32),
        ),
        in_specs=[vmem, vmem, hbm],
        out_specs=(vmem, vmem, hbm, vmem),
        scratch_shapes=[
            pltpu.VMEM(grades.shape, jnp.int32),
            pltpu.VMEM(e_shape, F32),
            dma((2 * n_col,)),
            dma((n_col,)),
            dma((n_pb,)),
            dma((n_pb,)),
            dma((3,)),
            dma((n_col, n_pb)),
        ],
        compiler_params=pltpu.CompilerParams(
            collective_id=0, has_side_effects=True, vmem_limit_bytes=56 * 2**20
        ),
        name="front",
    )(q, c, grades)


def merge_kernel(n_col, columns, parts_ref, all_ref, s_ref, got, mine, send, recv, send2, recv2):
    me = lax.axis_index("col")
    p = lax.axis_index("pb")
    others = [lax.rem(me + d, n_col) for d in range(1, n_col)]
    greet([dev(p, o) for o in others])
    G = GRADES
    for k in range(n_col):
        parts = [parts_ref[k, h] for h in range(parts_ref.shape[1])]
        top = parts[0][:G]
        for part in parts[1:]:
            top = jnp.maximum(top, part[:G])
        mass = sum(part[G : 2 * G] * jnp.exp(part[:G] - top) for part in parts)
        s_ref[k] = jnp.concatenate([top, mass, sum(part[2 * G :] for part in parts)], axis=0)
    copies = []
    for d, o in enumerate(others):
        copy = remote(s_ref.at[o], got.at[me], send.at[d], recv.at[me], dev(p, o))
        copy.start()
        copies.append(copy)
    got[me] = s_ref[me]
    for o in others:
        remote(s_ref.at[o], got.at[o], send.at[0], recv.at[o], dev(p, o)).wait_recv()
    maxima = got[0][:G]
    for k in range(1, n_col):
        maxima = jnp.maximum(maxima, got[k][:G])
    masses = jnp.zeros_like(maxima)
    rest = jnp.zeros((STATS - 2 * G, maxima.shape[1]), F32)
    for k in range(n_col):
        block = got[k]
        masses = masses + block[G : 2 * G] * jnp.exp(block[:G] - maxima)
        rest = rest + block[2 * G :]
    mx = [maxima[b : b + 1] for b in range(G)]
    ms = [masses[b : b + 1] for b in range(G)]
    ct = [rest[b : b + 1] for b in range(G)]
    total = rest[G : G + 1]
    levels = []
    running = mx[0]
    seen = ct[0] * 0.0
    for b in range(G):
        running = jnp.maximum(running, mx[b])
        seen = seen + ct[b]
        summed = ms[0] * jnp.exp(mx[0] - running)
        for h in range(1, b + 1):
            summed = summed + ms[h] * jnp.exp(mx[h] - running)
        present = seen > 0.0
        levels.append(jnp.where(present, running + jnp.log(jnp.where(present, summed, 1.0)), running))
    weighted = ct[0] * levels[0]
    for b in range(1, G):
        weighted = weighted + ct[b] * levels[b]
    loss = (weighted - total) / columns
    factors = []
    for h in range(G):
        f = ct[h] * jnp.exp(mx[h] - levels[h])
        for b in range(h + 1, G):
            f = f + ct[b] * jnp.exp(mx[h] - levels[b])
        factors.append(f)
    pad = jnp.zeros((STATS - 2 * G - 1, loss.shape[1]), F32)
    mine[...] = jnp.concatenate(mx + factors + [loss, pad], axis=0)
    more = []
    for d, o in enumerate(others):
        copy = remote(mine, all_ref.at[me], send2.at[d], recv2.at[me], dev(p, o))
        copy.start()
        more.append(copy)
    all_ref[me] = mine[...]
    for o in others:
        remote(mine, all_ref.at[o], send2.at[0], recv2.at[o], dev(p, o)).wait_recv()
    for copy in copies + more:
        copy.wait_send()


def merge(stats, columns):
    n_col, _, _, rows = stats.shape
    shape = (n_col, STATS, rows)
    vmem = pl.BlockSpec(memory_space=pltpu.VMEM)
    return pl.pallas_call(
        functools.partial(merge_kernel, n_col, columns),
        out_shape=jax.ShapeDtypeStruct(shape, F32),
        in_specs=[vmem],
        out_specs=vmem,
        scratch_shapes=[
            pltpu.VMEM(shape, F32),
            pltpu.VMEM(shape, F32),
            pltpu.VMEM((STATS, rows), F32),
            pltpu.SemaphoreType.DMA((n_col,)),
            pltpu.SemaphoreType.DMA((n_col,)),
            pltpu.SemaphoreType.DMA((n_col,)),
            pltpu.SemaphoreType.DMA((n_col,)),
        ],
        compiler_params=pltpu.CompilerParams(collective_id=1, has_side_effects=True),
        name="merge",
    )(stats)


def slope_kernel(scaling, per, e_ref, g_ref, q_ref, c_ref, s_ref, f_ref, w_ref, qg_ref, cg_ref, acc):
    step = pl.program_id(0)
    G = GRADES
    rows = s_ref.shape[3]
    pieces = []
    n_pb = s_ref.shape[1]
    half = e_ref.shape[3]
    for k in range(per):
        merged, weight = f_ref[k], w_ref[k]
        factor = weight * merged[G : 2 * G]
        scaled = [factor * jnp.exp(s_ref[k, h, :G] - merged[:G]) for h in range(n_pb)]
        pad = jnp.zeros((rows - n_pb * G - 1, rows), F32)
        table = jnp.concatenate(scaled + [weight, pad], axis=0).T
        sections = []
        for h in range(n_pb):
            grades = g_ref[k * rows : (k + 1) * rows, h * half : (h + 1) * half]
            picked = jnp.broadcast_to(table[:, h * G : h * G + 1], grades.shape)
            for b in range(1, G):
                picked = jnp.where(grades == b, table[:, h * G + b : h * G + b + 1], picked)
            sections.append(picked * e_ref[k, h] - table[:, n_pb * G : n_pb * G + 1])
        slopes = jnp.concatenate(sections, axis=1)
        pieces.append(slopes.astype(BF16))
    slopes = jnp.concatenate(pieces, axis=0)
    part = jnp.dot(slopes, c_ref[...], preferred_element_type=F32) * scaling
    qg_ref[...] = part.astype(BF16).reshape(qg_ref.shape)
    term = lax.dot_general(
        slopes,
        q_ref[...].reshape(per * rows, -1),
        (((0,), (0,)), ((), ())),
        preferred_element_type=F32,
    )

    @pl.when(step == 0)
    def _():
        acc[...] = term

    @pl.when(step > 0)
    def _():
        acc[...] += term

    @pl.when(step == pl.num_programs(0) - 1)
    def _():
        cg_ref[...] = (acc[...] * scaling).astype(BF16)


def slope(expo, grades, q_all, c_block, stats, merged, weights, scaling):
    n, rows, width = q_all.shape
    cols = c_block.shape[0]
    per = 2 if n % 2 == 0 else 1
    block3 = lambda a, b: pl.BlockSpec((per, a, b), lambda i: (i, 0, 0))
    block4 = lambda a, b, c: pl.BlockSpec((per, a, b, c), lambda i: (i, 0, 0, 0))
    return pl.pallas_call(
        functools.partial(slope_kernel, scaling, per),
        grid=(n // per,),
        out_shape=(
            jax.ShapeDtypeStruct((n, rows, width), BF16),
            jax.ShapeDtypeStruct((cols, width), BF16),
        ),
        in_specs=[
            block4(*expo.shape[1:]),
            pl.BlockSpec((per * rows, cols), lambda i: (i, 0)),
            block3(rows, width),
            pl.BlockSpec((cols, width), lambda i: (0, 0)),
            block4(*stats.shape[1:]),
            block3(STATS, rows),
            block3(1, rows),
        ],
        out_specs=(block3(rows, width), pl.BlockSpec((cols, width), lambda i: (0, 0))),
        scratch_shapes=[pltpu.VMEM((cols, width), F32)],
        compiler_params=pltpu.CompilerParams(vmem_limit_bytes=48 * 2**20),
        name="slope",
    )(expo, grades, q_all, c_block, stats, merged, weights)


def scatter_kernel(
    n_col, n_pb, qg, cg, q_out, c_out,
    core_got, acc, mid_got, out_got, c_got,
    core_send, core_recv, mid_send, mid_recv, out_send, out_recv, c_send, c_recv,
):
    at = Place(n_col, n_pb)
    greet(at.peers())
    copies = []

    def push(*args):
        copy = remote(*args)
        copy.start()
        copies.append(copy)

    for d in range(1, n_pb):
        other = lax.rem(at.p + d, n_pb)
        push(cg.at[other], c_got.at[d - 1], c_send.at[d], c_recv.at[d - 1], dev(other, at.me))
    order = sorted(range(1, at.outs), key=lambda d: min(d, at.outs - d)) + [0]
    far = [(do, dm) for do in order for dm in range(1, at.mids)] + [(do, 0) for do in order]
    slot = {pair: k for k, pair in enumerate(far)}
    for do, dm in far:
        k = slot[do, dm]
        if at.cores > 1:
            push(
                qg.at[at.index(do, dm, 1)], core_got.at[k], core_send.at[k], core_recv.at[k],
                dev(at.p, at.index(0, 0, 1)),
            )

    def core_sum(do, dm):
        k = slot[do, dm]
        own = qg[at.index(do, dm, 0)].astype(F32)
        if at.cores > 1:
            remote(core_got.at[k], core_got.at[k], core_send.at[k], core_recv.at[k], dev(at.p, at.me)).wait_recv()
            own = own + core_got[k].astype(F32)
        return own

    for do in order:
        for dm in range(1, at.mids):
            k = slot[do, dm]
            acc[k] = core_sum(do, dm).astype(BF16)
            push(acc.at[k], mid_got.at[k], mid_send.at[k], mid_recv.at[k], dev(at.p, at.index(0, dm, 0)))
    for do in order:
        k = slot[do, 0]
        acc[k] = core_sum(do, 0).astype(BF16)
    for do in order:
        k = slot[do, 0]
        total = acc[k].astype(F32)
        for dm in range(1, at.mids):
            j = slot[do, dm]
            remote(acc.at[j], mid_got.at[j], mid_send.at[j], mid_recv.at[j], dev(at.p, at.me)).wait_recv()
            total = total + mid_got[j].astype(F32)
        if do:
            acc[k] = total.astype(BF16)
            push(acc.at[k], out_got.at[do - 1], out_send.at[do - 1], out_recv.at[do - 1], dev(at.p, at.index(do, 0, 0)))
    for d in range(1, at.outs):
        remote(acc.at[0], out_got.at[d - 1], out_send.at[d - 1], out_recv.at[d - 1], dev(at.p, at.me)).wait_recv()
        total = total + out_got[d - 1].astype(F32)
    q_out[...] = total.astype(BF16)
    for d in range(1, n_pb):
        remote(cg.at[0], c_got.at[d - 1], c_send.at[d], c_recv.at[d - 1], dev(at.p, at.me)).wait_recv()
    half = 128
    for r in range(0, c_out.shape[0], half):
        rows = pl.ds(r, half)
        c_total = cg[at.p, rows].astype(F32)
        for d in range(1, n_pb):
            c_total = c_total + c_got[d - 1, rows].astype(F32)
        c_out[rows] = c_total.astype(BF16)
    for copy in copies:
        copy.wait_send()


def scatter(qg, cg):
    n_col, rows, width = qg.shape
    n_pb, crows, _ = cg.shape
    vmem = pl.BlockSpec(memory_space=pltpu.VMEM)
    block = (rows, width)
    dma = pltpu.SemaphoreType.DMA
    return pl.pallas_call(
        functools.partial(scatter_kernel, n_col, n_pb),
        out_shape=(jax.ShapeDtypeStruct(block, BF16), jax.ShapeDtypeStruct((crows, width), BF16)),
        in_specs=[vmem, vmem],
        out_specs=(vmem, vmem),
        scratch_shapes=[
            pltpu.VMEM((n_col, *block), BF16),
            pltpu.VMEM((n_col, *block), BF16),
            pltpu.VMEM((n_col, *block), BF16),
            pltpu.VMEM((n_col, *block), BF16),
            pltpu.VMEM((max(n_pb - 1, 1), crows, width), BF16),
        ]
        + [dma((n_col,))] * 6
        + [dma((n_pb,))] * 2,
        compiler_params=pltpu.CompilerParams(
            collective_id=2, has_side_effects=True, vmem_limit_bytes=60 * 2**20
        ),
        name="scatter",
    )(qg, cg)


def local(queries, candidates, grades, query_weights):
    n_col, n_pb = lax.axis_size("col"), lax.axis_size("pb")
    width = queries.shape[1]
    rows = queries.shape[0]
    scaling = 1.0 / math.sqrt(width)
    q_all, c_all, expo, stats = front(queries, candidates, grades, n_col, n_pb, scaling)
    c_block = c_all.reshape(-1, width)
    merged = merge(stats, grades.shape[1] * n_col)
    losses = merged[:, 2 * GRADES].reshape(-1)
    weights = query_weights.reshape(n_col, 1, rows)
    qg, cg = slope(expo, grades, q_all, c_block, stats, merged, weights, scaling)
    query_grad, cand_grad = scatter(qg, cg.reshape(n_pb, -1, width))
    return (losses, query_grad, cand_grad)


def solution(mesh):
    in_specs = (P(("pb", "col"), None), P(("col", "pb"), None), P("pb", "col"), P("pb"))
    out_specs = (P("pb"), P(("pb", "col"), None), P(("col", "pb"), None))
    return jax.shard_map(local, mesh=mesh, in_specs=in_specs, out_specs=out_specs, check_vma=False)
```

profile of v0, /device:TPU:0, one launch (start us, length us, event | category | flops | bytes accessed | tf_op | source)
XLA Modules:
  0.0 148.4 jit_solution(17794237491519640038)
XLA Ops:
  0.6 0.0 copy-start.4
  0.6 59.4 %front.1 = (bf16[16,128,1024]{2,1,0:T(8,128)(2,1)}, bf16[2,512,1024]{2,1,0:T(8,128)(2,1)}, f32[16,2,128,512]{3,2,1,0:T(8,128)}, f32[16,2,16,128]{3,2,1,0:T(8,128)}) custom-call(bf16[128,1024]{1,0:T(8,128)(2,1)} %q_ref.1, bf16[512,1024]{1,0:T(8,128)(2,1)} %c_ref.1, s32[2048,1024]{1,0:T(8,128)} %g_ref.1), custom_call_target="tpu_custom_call" | custom-call | tf_op jit(solution)/shard_map/front/pallas_call | solution.py:225
  60.1 15.8 %merge.1.f_ref = f32[16,16,128]{2,1,0:T(8,128)} custom-call(f32[16,2,16,128]{3,2,1,0:T(8,128)} %get-tuple-element.11.parts_ref.s_ref), custom_call_target="tpu_custom_call" | custom-call | tf_op jit(solution)/shard_map/merge/pallas_call | solution.py:325
  75.8 0.0 copy-done.4
  75.8 0.0 copy-start.1
  75.8 1.6 %copy-done.1 = bf16[2,512,1024]{2,1,0:T(8,128)(2,1)S(1)} copy-done((bf16[2,512,1024]{2,1,0:T(8,128)(2,1)S(1)}, bf16[2,512,1024]{2,1,0:T(8,128)(2,1)}, u32[]{:S(2)}) %copy-start.1) | copy-done | bytes 2097176
  77.4 0.0 copy-start.2
  77.4 0.9 copy-done.2
  78.4 0.0 copy-start.3
  78.4 0.9 copy-done.3
  79.3 21.1 %slope.1 = (bf16[16,128,1024]{2,1,0:T(8,128)(2,1)}, bf16[1024,1024]{1,0:T(8,128)(2,1)S(1)}) custom-call(f32[16,2,128,512]{3,2,1,0:T(8,128)} %get-tuple-element.12.e_ref, s32[2048,1024]{1,0:T(8,128)} %g_ref.1, bf16[16,128,1024]{2,1,0:T(8,128)(2,1)} %get-tuple-element.13.q_ref, bf16[1024,1024]{1,0:T(8,128)(2,1)S(1)} %bitcast.5, ...), custom_call_target="tpu_custom_call" | custom-call | tf_op jit(solution)/shard_map/slope/pallas_call | solution.py:395
  100.4 0.0 copy-start
  100.4 1.3 copy-done
  101.8 0.6 slice.3
  102.4 42.1 %scatter.1 = (bf16[128,1024]{1,0:T(8,128)(2,1)}, bf16[512,1024]{1,0:T(8,128)(2,1)}) custom-call(bf16[16,128,1024]{2,1,0:T(8,128)(2,1)} %get-tuple-element.15.qg, bf16[2,512,1024]{2,1,0:T(8,128)(2,1)} %bitcast.4), custom_call_target="tpu_custom_call" | custom-call | tf_op jit(solution)/shard_map/scatter/pallas_call | solution.py:495
  144.5 1.7 %copy.9 = bf16[128,1024]{1,0:T(8,128)(2,1)} copy(bf16[128,1024]{1,0:T(8,128)(2,1)} %get-tuple-element.23) | data formatting | bytes 524288
  146.1 2.3 %copy.10 = bf16[512,1024]{1,0:T(8,128)(2,1)} copy(bf16[512,1024]{1,0:T(8,128)(2,1)} %get-tuple-element.24) | data formatting | bytes 2097152
Async XLA Ops:
  0.6 75.2 %copy-start.4 = (f32[2048]{0:T(1024)S(1)}, f32[2048]{0:T(1024)}, u32[]{:S(2)}) copy-start(f32[2048]{0:T(1024)} %param.7) | copy-start | bytes 24580
  75.8 1.6 %copy-start.1 = (bf16[2,512,1024]{2,1,0:T(8,128)(2,1)S(1)}, bf16[2,512,1024]{2,1,0:T(8,128)(2,1)}, u32[]{:S(2)}) copy-start(bf16[2,512,1024]{2,1,0:T(8,128)(2,1)} %get-tuple-element.14) | copy-start | bytes 6291460
  77.4 0.9 copy-start.2
  78.4 0.9 copy-start.3
  100.4 1.3 copy-start
where the time goes:
time: 149 us; the launch traced here: 148 us
  Pallas kernels  138 us (93%)
  local copies, waits for them, and re-layouts  9.33 us (6%)
    pallas_call x1, Pallas kernels, front(): pl.pallas_call(functools.partial(front_kernel, n_col, n_pb, scaling), out...  59.4 us
    pallas_call x1, Pallas kernels, scatter(): pl.pallas_call(functools.partial(scatter_kernel, n_col, n_pb), out_shape=...  42.1 us
    pallas_call x1, Pallas kernels, slope(): pl.pallas_call(functools.partial(slope_kernel, scaling, per), grid=(n //...  21.1 us
    pallas_call x1, Pallas kernels, merge(): pl.pallas_call(functools.partial(merge_kernel, n_col, columns), out_shape...  15.8 us
    unnamed x12, local copies, waits for them, and re-layouts  8.72 us

commit v1 on v0

v1 whole, which is shorter than its diff:
```python
import functools
import math

import jax
import jax.numpy as jnp
from jax import lax
from jax.experimental import pallas as pl
from jax.experimental.pallas import tpu as pltpu
from jax.sharding import PartitionSpec as P

GRADES = 5
STATS = 16
LOWEST = -1e30
LANES = 128
SUBS = 2
MESH = pl.DeviceIdType.MESH
F32 = jnp.float32
BF16 = jnp.bfloat16
LOG2E = math.log2(math.e)
LN2 = math.log(2.0)


class Place:
    def __init__(self, n_col, n_pb):
        assert n_col % 4 == 0
        self.n_col, self.n_pb = n_col, n_pb
        self.cores = self.mids = 2
        self.chips = n_col // 2
        self.outs = n_col // 4
        self.me = lax.axis_index("col")
        self.p = lax.axis_index("pb")
        self.core = lax.rem(self.me, 2)
        self.mid = lax.rem(self.me // 2, 2)
        self.out = self.me // 4

    def chip(self, out, dm):
        return out * 2 + lax.rem(self.mid + dm, 2)

    def block(self, out, dm, dc):
        return self.chip(out, dm) * 2 + lax.rem(self.core + dc, 2)

    def dev(self, col):
        return {"pb": self.p, "col": col}

    def visit(self, k):
        side = jnp.minimum(self.out, self.outs - 1 - self.out)
        near = (k + 1) // 2 * (2 * lax.rem(k, 2) - 1)
        far = (k - side) * jnp.where(2 * self.out < self.outs, 1, -1)
        return self.out + jnp.where(k <= 2 * side, near, far)

    def item(self, t):
        odd = (lax.rem(t, 2) == 1) & (t < self.chips - 1)
        first = t == 0
        v = jnp.where(odd, self.outs - 1 - (t + 1) // 2, self.outs - 1 - (t - 1) // 2)
        v = jnp.where(first, self.outs - 1, v)
        dm = jnp.where(odd | first, 1, 0)
        return self.visit(v), dm


def remote(src, dst, send, recv, device):
    return pltpu.make_async_remote_copy(
        src_ref=src, dst_ref=dst, send_sem=send, recv_sem=recv, device_id=device, device_id_type=MESH
    )


def span(block, size):
    return pl.ds(pl.multiple_of(block * size, size), size)


def stats_table(s, g):
    rows = s.shape[0]
    lane = lax.broadcasted_iota(jnp.int32, (rows, LANES), 1)
    tops = [jnp.max(jnp.where(g <= b, s, LOWEST), axis=1, keepdims=True) for b in range(GRADES - 1)]
    tops.append(jnp.max(s, axis=1, keepdims=True))
    picked = tops[-1]
    for b in range(GRADES - 2, -1, -1):
        picked = jnp.where(g <= b, tops[b], picked)
    e = jnp.exp2(s - picked)
    sums = [jnp.sum(jnp.where(g <= b, e, 0.0), axis=1, keepdims=True) for b in range(GRADES - 1)]
    sums.append(jnp.sum(e, axis=1, keepdims=True))
    table = jnp.where(lane == 2 * GRADES, jnp.sum(s, axis=1, keepdims=True), 0.0)
    for b in range(GRADES):
        table = jnp.where(lane == b, tops[b], table)
        table = jnp.where(lane == GRADES + b, sums[b], table)
    return table


def count_table(g):
    rows, cols = g.shape
    assert cols % LANES == 0 and cols // LANES < 16 and cols < 4096
    code = jnp.zeros((rows, LANES), jnp.int32)
    for k in range(0, cols, LANES):
        code = code + jnp.left_shift(1, g[:, k : k + LANES] * 4)
    lane = lax.broadcasted_iota(jnp.int32, (rows, LANES), 1)
    table = jnp.zeros((rows, LANES), F32)
    for b in range(0, GRADES - 1, 2):
        low = jnp.right_shift(code, 4 * b) & 15
        high = jnp.right_shift(code, 4 * b + 4) & 15
        pair = jnp.sum((low + high * 4096).astype(F32), axis=1, keepdims=True)
        high = jnp.floor(pair * (1.0 / 4096.0))
        table = jnp.where(lane == b, pair - high * 4096.0, table)
        table = jnp.where(lane == b + 1, high, table)
    return table


def finish(got, n_col, cols, columns):
    G = GRADES
    tops = got[0][:G]
    for k in range(1, n_col):
        tops = jnp.maximum(tops, got[k][:G])
    masses = jnp.zeros_like(tops)
    rest = jnp.zeros((STATS - 2 * G, tops.shape[1]), F32)
    for k in range(n_col):
        block = got[k]
        masses = masses + block[G : 2 * G] * jnp.exp2(block[:G] - tops)
        rest = rest + block[2 * G :]
    top = [tops[b : b + 1] for b in range(G)]
    mass = [masses[b : b + 1] for b in range(G)]
    total = rest[:1]
    count = [rest[b + 1 : b + 2] for b in range(G - 1)]
    count.append(float(cols * n_col) - (count[0] + count[1] + count[2] + count[3]))
    levels = []
    seen = jnp.zeros_like(total)
    summed = seen
    weighted = seen
    for b in range(G):
        seen = seen + count[b]
        summed = mass[b] if b == 0 else mass[b] + summed * jnp.exp2(top[b - 1] - top[b])
        present = seen > 0.0
        level = jnp.where(present, top[b] + jnp.log(jnp.where(present, summed, 1.0)) * LOG2E, top[b])
        levels.append(level)
        weighted = weighted + count[b] * level
    loss = (weighted - total) * (LN2 / columns)
    offsets = [None] * G
    factor = seen * 0.0
    for b in range(G - 1, -1, -1):
        own = count[b] * jnp.exp2(top[b] - levels[b])
        factor = own if b == G - 1 else own + factor * jnp.exp2(top[b] - top[b + 1])
        offsets[b] = jnp.log(jnp.maximum(factor, 1e-37)) * LOG2E - top[b]
    pad = jnp.zeros((8 - G - 1, loss.shape[1]), F32)
    return jnp.concatenate(offsets + [loss, pad], axis=0)


def kernel(
    n_col, n_pb, pieces, scaling, columns,
    q_hbm, c_hbm, g_hbm, w_ref, loss_ref, q_out, c_out,
    q_all, c_all, g_all, s_all, slopes, tables, counts, stats, got, mine, merged,
    q_part, core_got, y_got, z_got, z_part, acc, c_part, c_own, c_got,
    own_sem, g_sem, q_send, q_recv, c_send, c_recv, s_send, s_recv, m_send, m_recv,
    k_send, k_recv, y_send, y_recv, z_send, z_recv, x_send, x_recv,
):
    at = Place(n_col, n_pb)
    rows, width = q_hbm.shape
    half = c_hbm.shape[0]
    cols = half * n_pb
    pair = 2 * rows
    sub = rows // SUBS
    outs, chips = at.outs, at.chips
    G = GRADES
    wide = half // pieces
    far_parts = [(d, s) for s in range(pieces) for d in range(1, n_pb)]
    n_far = len(far_parts)

    own_q = pltpu.make_async_copy(q_hbm, q_all.at[span(at.me, rows)], own_sem.at[0])
    own_c = pltpu.make_async_copy(c_hbm, c_all.at[span(at.p, half)], own_sem.at[1])
    own_q.start()
    own_c.start()

    def grades_in(k, start):
        for dm in range(2):
            chip = at.chip(at.visit(k), dm)
            copy = pltpu.make_async_copy(g_hbm.at[span(chip, pair)], g_all.at[span(chip, pair)], g_sem.at[chip])
            copy.start() if start else copy.wait()

    for k in range(outs):
        grades_in(k, True)
    barrier = pltpu.get_barrier_semaphore()
    for d in range(1, n_col):
        pl.semaphore_signal(
            barrier, inc=1, device_id=at.dev(lax.rem(at.me + d, n_col)), device_id_type=MESH
        )
    for d in range(1, n_pb):
        pl.semaphore_signal(
            barrier, inc=1, device_id={"pb": lax.rem(at.p + d, n_pb), "col": at.me}, device_id_type=MESH
        )
    pl.semaphore_wait(barrier, n_col + n_pb - 2)

    def q_span(block, s):
        return pl.ds(pl.multiple_of(block * rows + s * sub, sub), sub)

    def q_copy(block, s, t, col):
        ref = q_all.at[q_span(block, s)]
        return remote(ref, ref, q_send.at[block, t, s], q_recv.at[block, s], at.dev(col))

    def forward(k, dm, act):
        out = at.visit(k)
        block = at.block(out, dm, 0)
        for s in range(SUBS):
            if act and not (isinstance(k, int) and k == 0 and dm == 0):
                q_copy(block, s, 0, at.me).wait_recv()

            def go(t, col):
                copy = q_copy(block, s, t, col)
                copy.start() if act else copy.wait_send()

            if dm == 0:
                @pl.when((out <= at.out) & (at.out < outs - 1))
                def _():
                    go(0, at.block(at.out + 1, 0, 0))

                @pl.when((out >= at.out) & (at.out > 0))
                def _():
                    go(1, at.block(at.out - 1, 0, 0))

                go(2, at.block(at.out, 1, 0))
            go(3, at.block(at.out, 0, 1))

    def partner(k, dm):
        block = at.block(at.visit(k), dm, 1)
        for s in range(SUBS):
            q_copy(block, s, 0, at.me).wait_recv()

    def c_copy(d, s):
        ref = c_all.at[pl.ds(pl.multiple_of(at.p * half + s * wide, wide), wide)]
        other = lax.rem(at.p + d, n_pb)
        return remote(ref, ref, c_send.at[d, s], c_recv.at[at.p, s], {"pb": other, "col": at.me})

    def c_arrived(d, s):
        other = lax.rem(at.p + d, n_pb)
        ref = c_all.at[pl.ds(pl.multiple_of(other * half + s * wide, wide), wide)]
        remote(ref, ref, c_send.at[d, s], c_recv.at[other, s], at.dev(at.me)).wait_recv()

    own_q.wait()
    forward(0, 0, True)
    own_c.wait()
    for d, s in far_parts:
        c_copy(d, s).start()

    def score(k, dm, start, size, part):
        chip = at.chip(at.visit(k), dm)
        columns_ = pl.ds(pl.multiple_of(start, size), size)
        rr = span(chip, pair)
        s = lax.dot_general(
            q_all[rr], c_all[columns_], (((1,), (1,)), ((), ())), preferred_element_type=F32
        ) * (scaling * LOG2E)
        s_all[rr, columns_] = s
        for c in range(2):
            block = chip * 2 + c
            g = g_all[span(block, rows), columns_]
            tables[block, part] = stats_table(s[c * rows : (c + 1) * rows], g).T[:STATS]

    def near(k, dm):
        score(k, dm, at.p * half, half, 0)

    def far(k, dm, r):
        d, s = far_parts[r] if isinstance(r, int) else (1 + lax.rem(r, n_pb - 1), r // (n_pb - 1))
        start = lax.rem(at.p + d, n_pb) * half + s * wide
        score(k, dm, start, wide, r + 1)

    def count(block, carry):
        counts[block] = count_table(g_all[span(block, rows), :]).T[:8]
        return carry

    partner(0, 0)
    for k in range(outs):
        grades_in(k, False)
    early = n_far // 2

    def step(u, carry):
        @pl.when((u > 0) & (u < outs))
        def _():
            forward(u, 0, True)

        @pl.when((u > 0) & (u <= outs))
        def _():
            forward(u - 1, 1, True)
            partner(u - 1, 1)
            near(u - 1, 1)

        @pl.when((u > 0) & (u < outs))
        def _():
            partner(u, 0)

        @pl.when(u < outs)
        def _():
            near(u, 0)

        @pl.when(u == 0)
        def _():
            lax.fori_loop(0, n_col, count, 0)

        @pl.when(u >= 2)
        def _():
            @pl.when(u == 2)
            def _():
                for r in range(early):
                    c_arrived(*far_parts[r])

            def body(j, c):
                far(u - 2, lax.rem(j, 2), j // 2)
                return c

            lax.fori_loop(0, 2 * early, body, 0)

        return carry

    lax.fori_loop(0, outs + 2, step, 0)
    for r in range(early, n_far):
        c_arrived(*far_parts[r])

    def stat_copy(block):
        return remote(stats.at[block], got.at[at.me], s_send.at[block], s_recv.at[at.me], at.dev(block))

    def last(j, carry):
        k, dm = outs - 1 - j // 2, 1 - lax.rem(j, 2)

        def body(r, c):
            far(k, dm, r)
            return c

        lax.fori_loop(early, n_far, body, 0)
        for c in range(2):
            block = at.chip(at.visit(k), dm) * 2 + c
            parts = [tables[block, h] for h in range(n_far + 1)]
            top = parts[0][:G]
            for part in parts[1:]:
                top = jnp.maximum(top, part[:G])
            mass = jnp.zeros_like(top)
            total = jnp.zeros((1, rows), F32)
            for part in parts:
                upto = part[G : 2 * G]
                own = jnp.concatenate([upto[:1], upto[1:] - upto[:-1]], axis=0)
                mass = mass + own * jnp.exp2(part[:G] - top)
                total = total + part[2 * G : 2 * G + 1]
            pad = jnp.zeros((1, rows), F32)
            stats[block] = jnp.concatenate([top, mass, total, counts[block, :4], pad], axis=0)

            @pl.when(block != at.me)
            def _():
                stat_copy(block).start()

        return carry

    lax.fori_loop(0, chips, last, 0)

    others = [lax.rem(at.me + d, n_col) for d in range(1, n_col)]
    got[at.me] = stats[at.me]
    for o in others:
        remote(stats.at[o], got.at[o], s_send.at[o], s_recv.at[o], at.dev(at.me)).wait_recv()
    mine[...] = finish(got, n_col, cols, columns)

    def merged_copy(o):
        return remote(mine, merged.at[at.me], m_send.at[o], m_recv.at[at.me], at.dev(o))

    for o in others:
        merged_copy(o).start()
    merged[at.me] = mine[...]
    for o in others:
        remote(mine, merged.at[o], m_send.at[o], m_recv.at[o], at.dev(at.me)).wait_recv()

    step_rows = min(64, rows)

    def slope(block):
        table = jnp.concatenate(
            [merged[block][: G + 1], w_ref[pl.ds(block, 1), :], jnp.zeros((rows - G - 2, rows), F32)], axis=0
        ).T
        loss_ref[pl.ds(block, 1), :] = merged[block][G : G + 1]
        for r in range(0, rows, step_rows):
            rr = pl.ds(pl.multiple_of(block * rows + r, step_rows), step_rows)
            t = table[r : r + step_rows]
            g = g_all[rr, :]
            off = jnp.broadcast_to(t[:, G - 1 : G], g.shape)
            for b in range(G - 2, -1, -1):
                off = jnp.where(g <= b, t[:, b : b + 1], off)
            w = t[:, G + 1 : G + 2]
            slopes[rr, :] = (w * jnp.exp2(s_all[rr, :] + off) - w).astype(BF16)

    def k_copy(chip):
        return remote(
            q_part.at[chip, lax.rem(at.core + 1, 2)], core_got.at[chip], k_send.at[chip], k_recv.at[chip],
            at.dev(at.block(at.out, 0, 1)),
        )

    def q_grad(t):
        out, dm = at.item(t)
        chip = at.chip(out, dm)
        part = jnp.dot(slopes[span(chip, pair), :], c_all[...], preferred_element_type=F32) * scaling
        q_part[chip] = part.astype(BF16).reshape(2, rows, width)
        k_copy(chip).start()

    def sub_rows(s):
        return pl.ds(s * sub, sub)

    def y_copy(out, s):
        return remote(
            q_part.at[at.chip(out, 1), at.core, sub_rows(s)], y_got.at[out, sub_rows(s)],
            y_send.at[out, s], y_recv.at[out, s], at.dev(at.block(at.out, 1, 0)),
        )

    def cross(out):
        chip = at.chip(out, 1)
        k_copy(chip).wait_recv()
        for s in range(SUBS):
            rr = sub_rows(s)
            both = q_part[chip, at.core, rr].astype(F32) + core_got[chip, rr].astype(F32)
            q_part[chip, at.core, rr] = both.astype(BF16)
            y_copy(out, s).start()

    def z_copy(out, s):
        toward = jnp.where(out > at.out, at.out + 1, at.out - 1)
        slot = jnp.where((out < at.out) & (toward == out), outs, out)
        return remote(
            z_part.at[out, sub_rows(s)], z_got.at[slot, sub_rows(s)],
            z_send.at[out, s], z_recv.at[slot, s], at.dev(at.block(toward, 0, 0)),
        )

    def z_add(slot, s):
        ref = z_got.at[slot, sub_rows(s)]
        remote(ref, ref, z_send.at[0, s], z_recv.at[slot, s], at.dev(at.me)).wait_recv()
        acc[...] += z_got[slot, sub_rows(s)].astype(F32)

    def gather_row(out, s):
        chip = at.chip(out, 0)
        rr = sub_rows(s)
        ref = y_got.at[out, rr]
        remote(ref, ref, y_send.at[out, s], y_recv.at[out, s], at.dev(at.me)).wait_recv()
        acc[...] = (
            q_part[chip, at.core, rr].astype(F32)
            + core_got[chip, rr].astype(F32)
            + y_got[out, rr].astype(F32)
        )

    def chain(v):
        out = at.visit(v)
        k_copy(at.chip(out, 0)).wait_recv()
        behind = ((out > at.out) & (at.out > 0)) | ((out < at.out) & (at.out < outs - 1))
        for s in range(SUBS):
            gather_row(out, s)

            @pl.when(behind)
            def _():
                z_add(out, s)

            z_part[out, sub_rows(s)] = acc[...].astype(BF16)
            z_copy(out, s).start()

    chunk = min(LANES, half)
    per = half // chunk
    n_x = per * (n_pb - 1)

    def x_copy(r):
        d, j = 1 + r // per, lax.rem(r, per)
        other = lax.rem(at.p + d, n_pb)
        rr = pl.ds(pl.multiple_of(j * chunk, chunk), chunk)
        return remote(
            c_part.at[r], c_got.at[d - 1, rr], x_send.at[r], x_recv.at[r], {"pb": other, "col": at.me}
        )

    def c_grad(start):
        return lax.dot_general(
            slopes[:, pl.ds(pl.multiple_of(start, chunk), chunk)], q_all[...],
            (((0,), (0,)), ((), ())), preferred_element_type=F32,
        ) * scaling

    def c_far(r):
        other = lax.rem(at.p + 1 + r // per, n_pb)
        c_part[r] = c_grad(other * half + lax.rem(r, per) * chunk).astype(BF16)
        x_copy(r).start()

    def slope_step(i, carry):
        out, dm = at.item(i)
        for c in range(2):
            slope(at.chip(out, dm) * 2 + c)

        @pl.when(i == 0)
        def _():
            q_grad(0)

        @pl.when(i == 2)
        def _():
            cross(at.visit(outs - 1))

        return carry

    lax.fori_loop(0, chips, slope_step, 0)

    def grad_step(j, carry):
        @pl.when(j < n_x)
        def _():
            c_far(j)

        @pl.when(j + 1 < chips)
        def _():
            q_grad(j + 1)

        @pl.when((j >= 1) & (lax.rem(j, 2) == 1) & (j < chips - 1))
        def _():
            cross(at.item(j)[0])

        return carry

    lax.fori_loop(0, max(n_x, chips - 1), grad_step, 0)

    def c_near(j, carry):
        c_own[pl.ds(pl.multiple_of(j * chunk, chunk), chunk)] = c_grad(at.p * half + j * chunk)
        return carry

    def chain_step(i, carry):
        chain(outs - 1 - i)

        @pl.when(i == 0)
        def _():
            lax.fori_loop(0, per, c_near, 0)

        return carry

    lax.fori_loop(0, outs - 1, chain_step, 0)
    k_copy(at.chip(at.out, 0)).wait_recv()
    for s in range(SUBS):
        gather_row(at.out, s)

        @pl.when(at.out > 0)
        def _():
            z_add(at.out, s)

        @pl.when(at.out < outs - 1)
        def _():
            z_add(outs, s)

        q_out[sub_rows(s), :] = acc[...].astype(BF16)

    def c_finish(j, carry):
        rr = pl.ds(pl.multiple_of(j * chunk, chunk), chunk)
        total = c_own[rr]
        for d in range(1, n_pb):
            r = (d - 1) * per + j
            ref = c_got.at[d - 1, rr]
            remote(ref, ref, x_send.at[r], x_recv.at[r], at.dev(at.me)).wait_recv()
            total = total + c_got[d - 1, rr].astype(F32)
        c_out[rr] = total.astype(BF16)
        return carry

    lax.fori_loop(0, per, c_finish, 0)

    def drain(k, carry):
        for dm in range(2):
            forward(k, dm, False)
        out = at.visit(k)
        for dm in range(2):
            k_copy(at.chip(out, dm)).wait_send()
        for s in range(SUBS):
            y_copy(out, s).wait_send()

            @pl.when(k > 0)
            def _():
                z_copy(out, s).wait_send()

        return carry

    lax.fori_loop(0, outs, drain, 0)
    for d, s in far_parts:
        c_copy(d, s).wait_send()
    for o in others:
        stat_copy(o).wait_send()
        merged_copy(o).wait_send()
    lax.fori_loop(0, n_x, lambda r, c: (x_copy(r).wait_send(), c)[1], 0)


def local(queries, candidates, grades, query_weights):
    n_col, n_pb = lax.axis_size("col"), lax.axis_size("pb")
    rows, width = queries.shape
    half = candidates.shape[0]
    tall, cols = grades.shape
    scaling = 1.0 / math.sqrt(width)
    pieces = 2 if half % 256 == 0 else 1
    outs, chips = n_col // 4, n_col // 2
    chunk = min(LANES, half)
    n_x = half // chunk * (n_pb - 1)
    sub = rows // SUBS
    dma = pltpu.SemaphoreType.DMA
    vmem = pl.BlockSpec(memory_space=pltpu.VMEM)
    hbm = pl.BlockSpec(memory_space=pl.ANY)
    losses, query_grad, cand_grad = pl.pallas_call(
        functools.partial(kernel, n_col, n_pb, pieces, scaling, cols * n_col),
        out_shape=(
            jax.ShapeDtypeStruct((n_col, rows), F32),
            jax.ShapeDtypeStruct((rows, width), BF16),
            jax.ShapeDtypeStruct((half, width), BF16),
        ),
        in_specs=[hbm, hbm, hbm, vmem],
        out_specs=(vmem, vmem, vmem),
        scratch_shapes=[
            pltpu.VMEM((tall, width), BF16),
            pltpu.VMEM((cols, width), BF16),
            pltpu.VMEM((tall, cols), jnp.int32),
            pltpu.VMEM((tall, cols), F32),
            pltpu.VMEM((tall, cols), BF16),
            pltpu.VMEM((n_col, 1 + pieces * (n_pb - 1), STATS, rows), F32),
            pltpu.VMEM((n_col, 8, rows), F32),
            pltpu.VMEM((n_col, STATS, rows), F32),
            pltpu.VMEM((n_col, STATS, rows), F32),
            pltpu.VMEM((8, rows), F32),
            pltpu.VMEM((n_col, 8, rows), F32),
            pltpu.VMEM((chips, 2, rows, width), BF16),
            pltpu.VMEM((chips, rows, width), BF16),
            pltpu.VMEM((outs, rows, width), BF16),
            pltpu.VMEM((outs + 1, rows, width), BF16),
            pltpu.VMEM((outs, rows, width), BF16),
            pltpu.VMEM((sub, width), F32),
            pltpu.VMEM((n_x, chunk, width), BF16),
            pltpu.VMEM((half, width), F32),
            pltpu.VMEM((n_pb - 1, half, width), BF16),
            dma((2,)),
            dma((chips,)),
            dma((n_col, 4, SUBS)),
            dma((n_col, SUBS)),
            dma((n_pb, pieces)),
            dma((n_pb, pieces)),
            dma((n_col,)),
            dma((n_col,)),
            dma((n_col,)),
            dma((n_col,)),
            dma((chips,)),
            dma((chips,)),
            dma((outs, SUBS)),
            dma((outs, SUBS)),
            dma((outs, SUBS)),
            dma((outs + 1, SUBS)),
            dma((n_x,)),
            dma((n_x,)),
        ],
        compiler_params=pltpu.CompilerParams(
            collective_id=0, has_side_effects=True, vmem_limit_bytes=62 * 2**20
        ),
        name="listmle",
    )(queries, candidates, grades, query_weights.reshape(n_col, rows))
    return (losses.reshape(-1), query_grad, cand_grad)


def solution(mesh):
    in_specs = (P(("pb", "col"), None), P(("col", "pb"), None), P("pb", "col"), P("pb"))
    out_specs = (P("pb"), P(("pb", "col"), None), P(("col", "pb"), None))
    return jax.shard_map(local, mesh=mesh, in_specs=in_specs, out_specs=out_specs, check_vma=False)
```

time: 149 us -> 102 us (0.68)
  the two profiles are of different devices: /device:TPU:0 before, /device:TPU:24 now
where the time goes in v1:
time: 102 us; the launch traced here: 101 us
  Pallas kernels  94.6 us (93%)
  local copies, waits for them, and re-layouts  5.23 us (5%)
    pallas_call x1, Pallas kernels, local(): pl.pallas_call(functools.partial(kernel, n_col, n_pb, pieces, scaling, co...  94.6 us
    unnamed x3, local copies, waits for them, and re-layouts  5.23 us

profile of v1, /device:TPU:24, one launch (start us, length us, event | category | flops | bytes accessed | tf_op | source)
XLA Modules:
  0.0 100.5 jit_solution(8950016593611772178)
XLA Ops:
  0.6 94.6 %listmle.1 = (f32[16,128]{1,0:T(8,128)}, bf16[128,1024]{1,0:T(8,128)(2,1)}, bf16[512,1024]{1,0:T(8,128)(2,1)}) custom-call(bf16[128,1024]{1,0:T(8,128)(2,1)} %q_hbm.1, bf16[512,1024]{1,0:T(8,128)(2,1)} %c_hbm.1, s32[2048,1024]{1,0:T(8,128)} %g_hbm.1, f32[16,128]{1,0:T(8,128)} %bitcast.3), custom_call_target="tpu_custom_call" | custom-call | tf_op jit(solution)/shard_map/listmle/pallas_call | solution.py:583
  95.3 1.3 %copy.10 = f32[2048]{0:T(1024)} copy(f32[2048]{0:T(1024)} %bitcast.2) | data formatting | bytes 16384
  96.6 1.7 %copy.11 = bf16[128,1024]{1,0:T(8,128)(2,1)} copy(bf16[128,1024]{1,0:T(8,128)(2,1)} %get-tuple-element.13) | data formatting | bytes 524288
  98.2 2.3 %copy.12 = bf16[512,1024]{1,0:T(8,128)(2,1)} copy(bf16[512,1024]{1,0:T(8,128)(2,1)} %get-tuple-element.14) | data formatting | bytes 2097152

commit v2 on v1

--- a/solution.py
+++ b/solution.py
@@ -67,40 +67,17 @@
     return pl.ds(pl.multiple_of(block * size, size), size)
 
 
-def stats_table(s, g):
-    rows = s.shape[0]
-    lane = lax.broadcasted_iota(jnp.int32, (rows, LANES), 1)
-    tops = [jnp.max(jnp.where(g <= b, s, LOWEST), axis=1, keepdims=True) for b in range(GRADES - 1)]
-    tops.append(jnp.max(s, axis=1, keepdims=True))
-    picked = tops[-1]
+def statistics(s, g, put):
+    tops = [jnp.max(jnp.where(g <= b, s, LOWEST), axis=0, keepdims=True) for b in range(GRADES - 1)]
+    tops.append(jnp.max(s, axis=0, keepdims=True))
+    picked = jnp.broadcast_to(tops[-1], s.shape)
     for b in range(GRADES - 2, -1, -1):
         picked = jnp.where(g <= b, tops[b], picked)
     e = jnp.exp2(s - picked)
-    sums = [jnp.sum(jnp.where(g <= b, e, 0.0), axis=1, keepdims=True) for b in range(GRADES - 1)]
-    sums.append(jnp.sum(e, axis=1, keepdims=True))
-    table = jnp.where(lane == 2 * GRADES, jnp.sum(s, axis=1, keepdims=True), 0.0)
-    for b in range(GRADES):
-        table = jnp.where(lane == b, tops[b], table)
-        table = jnp.where(lane == GRADES + b, sums[b], table)
-    return table
-
-
-def count_table(g):
-    rows, cols = g.shape
-    assert cols % LANES == 0 and cols // LANES < 16 and cols < 4096
-    code = jnp.zeros((rows, LANES), jnp.int32)
-    for k in range(0, cols, LANES):
-        code = code + jnp.left_shift(1, g[:, k : k + LANES] * 4)
-    lane = lax.broadcasted_iota(jnp.int32, (rows, LANES), 1)
-    table = jnp.zeros((rows, LANES), F32)
-    for b in range(0, GRADES - 1, 2):
-        low = jnp.right_shift(code, 4 * b) & 15
-        high = jnp.right_shift(code, 4 * b + 4) & 15
-        pair = jnp.sum((low + high * 4096).astype(F32), axis=1, keepdims=True)
-        high = jnp.floor(pair * (1.0 / 4096.0))
-        table = jnp.where(lane == b, pair - high * 4096.0, table)
-        table = jnp.where(lane == b + 1, high, table)
-    return table
+    sums = [jnp.sum(jnp.where(g <= b, e, 0.0), axis=0, keepdims=True) for b in range(GRADES - 1)]
+    sums.append(jnp.sum(e, axis=0, keepdims=True))
+    for i, row in enumerate(tops + sums + [jnp.sum(s, axis=0, keepdims=True)]):
+        put(i, row)
 
 
 def finish(got, n_col, cols, columns):
@@ -141,10 +118,15 @@
     return jnp.concatenate(offsets + [loss, pad], axis=0)
 
 
+def far_parts_of(half, n_pb):
+    sizes = [half // 2, half // 4, half // 4] if half % 512 == 0 else [half]
+    return [(d, sum(sizes[:i]), n) for i, n in enumerate(sizes) for d in range(1, n_pb)]
+
+
 def kernel(
-    n_col, n_pb, pieces, scaling, columns,
+    n_col, n_pb, scaling, columns,
     q_hbm, c_hbm, g_hbm, w_ref, loss_ref, q_out, c_out,
-    q_all, c_all, g_all, s_all, slopes, tables, counts, stats, got, mine, merged,
+    q_all, c_all, g_raw, g_all, s_all, slopes, tables, counts, stats, got, mine, merged,
     q_part, core_got, y_got, z_got, z_part, acc, c_part, c_own, c_got,
     own_sem, g_sem, q_send, q_recv, c_send, c_recv, s_send, s_recv, m_send, m_recv,
     k_send, k_recv, y_send, y_recv, z_send, z_recv, x_send, x_recv,
@@ -152,28 +134,26 @@
     at = Place(n_col, n_pb)
     rows, width = q_hbm.shape
     half = c_hbm.shape[0]
-    cols = half * n_pb
-    pair = 2 * rows
+    tall, cols = g_hbm.shape
+    pair, quad = 2 * rows, 4 * rows
     sub = rows // SUBS
     outs, chips = at.outs, at.chips
     G = GRADES
-    wide = half // pieces
-    far_parts = [(d, s) for s in range(pieces) for d in range(1, n_pb)]
-    n_far = len(far_parts)
+    parts = far_parts_of(half, n_pb)
+    n_far = len(parts)
+    early = n_pb - 1
 
     own_q = pltpu.make_async_copy(q_hbm, q_all.at[span(at.me, rows)], own_sem.at[0])
     own_c = pltpu.make_async_copy(c_hbm, c_all.at[span(at.p, half)], own_sem.at[1])
     own_q.start()
     own_c.start()
-
-    def grades_in(k, start):
-        for dm in range(2):
-            chip = at.chip(at.visit(k), dm)
-            copy = pltpu.make_async_copy(g_hbm.at[span(chip, pair)], g_all.at[span(chip, pair)], g_sem.at[chip])
-            copy.start() if start else copy.wait()
-
-    for k in range(outs):
-        grades_in(k, True)
+    group = 8 * LANES
+    g_copies = [
+        pltpu.make_async_copy(g_hbm.at[pl.ds(h, group)], g_raw.at[pl.ds(h, group)], g_sem.at[h // group])
+        for h in range(0, tall, group)
+    ]
+    for copy in g_copies:
+        copy.start()
     barrier = pltpu.get_barrier_semaphore()
     for d in range(1, n_col):
         pl.semaphore_signal(
@@ -220,128 +200,155 @@
         for s in range(SUBS):
             q_copy(block, s, 0, at.me).wait_recv()
 
-    def c_copy(d, s):
-        ref = c_all.at[pl.ds(pl.multiple_of(at.p * half + s * wide, wide), wide)]
+    def c_copy(r):
+        d, first, n = parts[r]
+        ref = c_all.at[pl.ds(pl.multiple_of(at.p * half + first, n), n)]
         other = lax.rem(at.p + d, n_pb)
-        return remote(ref, ref, c_send.at[d, s], c_recv.at[at.p, s], {"pb": other, "col": at.me})
-
-    def c_arrived(d, s):
-        other = lax.rem(at.p + d, n_pb)
-        ref = c_all.at[pl.ds(pl.multiple_of(other * half + s * wide, wide), wide)]
-        remote(ref, ref, c_send.at[d, s], c_recv.at[other, s], at.dev(at.me)).wait_recv()
+        return remote(ref, ref, c_send.at[r], c_recv.at[r], {"pb": other, "col": at.me})
+
+    def c_arrived(r):
+        d, first, n = parts[r]
+        other = lax.rem(at.p + n_pb - d, n_pb)
+        ref = c_all.at[pl.ds(pl.multiple_of(other * half + first, n), n)]
+        remote(ref, ref, c_send.at[r], c_recv.at[r], at.dev(at.me)).wait_recv()
 
     own_q.wait()
     forward(0, 0, True)
     own_c.wait()
-    for d, s in far_parts:
-        c_copy(d, s).start()
-
-    def score(k, dm, start, size, part):
-        chip = at.chip(at.visit(k), dm)
-        columns_ = pl.ds(pl.multiple_of(start, size), size)
-        rr = span(chip, pair)
+    for r in range(n_far):
+        c_copy(r).start()
+
+    assert cols % LANES == 0 and cols // 8 < 256 and tall % group == 0
+    for h, copy in zip(range(0, tall, group), g_copies):
+        copy.wait()
+
+        def turn(k, codes, h=h):
+            cc = span(k, LANES)
+            word = g_raw[h : h + LANES, cc]
+            for i in range(1, 8):
+                word = word + jnp.left_shift(g_raw[h + i * LANES : h + (i + 1) * LANES, cc], 3 * i)
+            word = word.T
+            new = []
+            for i in range(8):
+                g = jnp.right_shift(word, 3 * i) & 7
+                g_all[cc, h + i * LANES : h + (i + 1) * LANES] = g
+                one = jnp.left_shift(1, g * 8)
+                code = codes[i]
+                for j in range(0, LANES, 8):
+                    code = code + one[j : j + 8]
+                new.append(code)
+            return tuple(new)
+
+        codes = lax.fori_loop(
+            0, cols // LANES, turn, tuple(jnp.zeros((8, LANES), jnp.int32) for _ in range(8))
+        )
+        for i in range(8):
+            for b in range(G - 1):
+                field = (jnp.right_shift(codes[i], 8 * b) & 255).astype(F32)
+                counts[b : b + 1, h + i * LANES : h + (i + 1) * LANES] = jnp.sum(field, axis=0, keepdims=True)
+
+    def score(chip, wide, start, size, part):
+        cc = pl.ds(pl.multiple_of(start, size), size)
         s = lax.dot_general(
-            q_all[rr], c_all[columns_], (((1,), (1,)), ((), ())), preferred_element_type=F32
+            c_all[cc], q_all[pl.ds(pl.multiple_of(chip * pair, wide), wide)],
+            (((1,), (1,)), ((), ())), preferred_element_type=F32,
         ) * (scaling * LOG2E)
-        s_all[rr, columns_] = s
-        for c in range(2):
-            block = chip * 2 + c
-            g = g_all[span(block, rows), columns_]
-            tables[block, part] = stats_table(s[c * rows : (c + 1) * rows], g).T[:STATS]
+        for x in range(0, wide, LANES):
+            qq = pl.ds(pl.multiple_of(chip * pair + x, LANES), LANES)
+            tile = s[:, x : x + LANES]
+            s_all[cc, qq] = tile
+
+            def put(i, row):
+                tables[chip + x // pair, part, i : i + 1, x % pair : x % pair + LANES] = row
+
+            statistics(tile, g_all[cc, qq], put)
 
     def near(k, dm):
-        score(k, dm, at.p * half, half, 0)
-
-    def far(k, dm, r):
-        d, s = far_parts[r] if isinstance(r, int) else (1 + lax.rem(r, n_pb - 1), r // (n_pb - 1))
-        start = lax.rem(at.p + d, n_pb) * half + s * wide
-        score(k, dm, start, wide, r + 1)
-
-    def count(block, carry):
-        counts[block] = count_table(g_all[span(block, rows), :]).T[:8]
-        return carry
+        score(at.chip(at.visit(k), dm), pair, at.p * half, half, 0)
+
+    def far(k, r):
+        d, first, n = parts[r]
+        score(2 * at.visit(k), quad, lax.rem(at.p + n_pb - d, n_pb) * half + first, n, r + 1)
+
+    def stat_copy(block):
+        return remote(stats.at[block], got.at[at.me], s_send.at[block], s_recv.at[at.me], at.dev(block))
+
+    def join(k):
+        for m in range(2):
+            chip = 2 * at.visit(k) + m
+            tabs = [tables[chip, h] for h in range(n_far + 1)]
+            top = tabs[0][:G]
+            for tab in tabs[1:]:
+                top = jnp.maximum(top, tab[:G])
+            mass = jnp.zeros_like(top)
+            total = jnp.zeros((1, pair), F32)
+            for tab in tabs:
+                upto = tab[G : 2 * G]
+                own = jnp.concatenate([upto[:1], upto[1:] - upto[:-1]], axis=0)
+                mass = mass + own * jnp.exp2(tab[:G] - top)
+                total = total + tab[2 * G : 2 * G + 1]
+            count = counts[:, span(chip, pair)][: G - 1]
+            whole = jnp.concatenate([top, mass, total, count, jnp.zeros((1, pair), F32)], axis=0)
+            for c in range(2):
+                block = chip * 2 + c
+                stats[block] = whole[:, c * rows : (c + 1) * rows]
+
+                @pl.when(block != at.me)
+                def _():
+                    stat_copy(block).start()
 
     partner(0, 0)
-    for k in range(outs):
-        grades_in(k, False)
-    early = n_far // 2
 
     def step(u, carry):
-        @pl.when((u > 0) & (u < outs))
+        @pl.when(u > 0)
         def _():
             forward(u, 0, True)
-
-        @pl.when((u > 0) & (u <= outs))
-        def _():
             forward(u - 1, 1, True)
             partner(u - 1, 1)
             near(u - 1, 1)
-
-        @pl.when((u > 0) & (u < outs))
-        def _():
             partner(u, 0)
 
-        @pl.when(u < outs)
-        def _():
-            near(u, 0)
-
-        @pl.when(u == 0)
-        def _():
-            lax.fori_loop(0, n_col, count, 0)
+        near(u, 0)
+
+        @pl.when(u == 2)
+        def _():
+            for r in range(early):
+                c_arrived(r)
 
         @pl.when(u >= 2)
         def _():
-            @pl.when(u == 2)
-            def _():
-                for r in range(early):
-                    c_arrived(*far_parts[r])
-
-            def body(j, c):
-                far(u - 2, lax.rem(j, 2), j // 2)
-                return c
-
-            lax.fori_loop(0, 2 * early, body, 0)
-
-        return carry
-
-    lax.fori_loop(0, outs + 2, step, 0)
+            for r in range(early):
+                far(u - 2, r)
+
+        return carry
+
+    lax.fori_loop(0, outs, step, 0)
+    if outs < 3:
+        for r in range(early):
+            c_arrived(r)
+    for k in range(max(outs - 2, 0), outs - 1):
+        for r in range(early):
+            far(k, r)
     for r in range(early, n_far):
-        c_arrived(*far_parts[r])
-
-    def stat_copy(block):
-        return remote(stats.at[block], got.at[at.me], s_send.at[block], s_recv.at[at.me], at.dev(block))
-
-    def last(j, carry):
-        k, dm = outs - 1 - j // 2, 1 - lax.rem(j, 2)
-
-        def body(r, c):
-            far(k, dm, r)
-            return c
-
-        lax.fori_loop(early, n_far, body, 0)
-        for c in range(2):
-            block = at.chip(at.visit(k), dm) * 2 + c
-            parts = [tables[block, h] for h in range(n_far + 1)]
-            top = parts[0][:G]
-            for part in parts[1:]:
-                top = jnp.maximum(top, part[:G])
-            mass = jnp.zeros_like(top)
-            total = jnp.zeros((1, rows), F32)
-            for part in parts:
-                upto = part[G : 2 * G]
-                own = jnp.concatenate([upto[:1], upto[1:] - upto[:-1]], axis=0)
-                mass = mass + own * jnp.exp2(part[:G] - top)
-                total = total + part[2 * G : 2 * G + 1]
-            pad = jnp.zeros((1, rows), F32)
-            stats[block] = jnp.concatenate([top, mass, total, counts[block, :4], pad], axis=0)
-
-            @pl.when(block != at.me)
-            def _():
-                stat_copy(block).start()
-
-        return carry
-
-    lax.fori_loop(0, chips, last, 0)
+        c_arrived(r)
+
+        def body(k, carry, r=r):
+            far(k, r)
+            return carry
+
+        lax.fori_loop(0, outs - 1, body, 0)
+
+    def joins(k, carry):
+        join(k)
+        return carry
+
+    lax.fori_loop(0, outs - 1, joins, 0)
+    forward(outs - 1, 1, True)
+    partner(outs - 1, 1)
+    near(outs - 1, 1)
+    for r in range(n_far):
+        far(outs - 1, r)
+    join(outs - 1)
 
     others = [lax.rem(at.me + d, n_col) for d in range(1, n_col)]
     got[at.me] = stats[at.me]
@@ -358,22 +365,27 @@
     for o in others:
         remote(mine, merged.at[o], m_send.at[o], m_recv.at[o], at.dev(at.me)).wait_recv()
 
-    step_rows = min(64, rows)
-
-    def slope(block):
-        table = jnp.concatenate(
-            [merged[block][: G + 1], w_ref[pl.ds(block, 1), :], jnp.zeros((rows - G - 2, rows), F32)], axis=0
-        ).T
-        loss_ref[pl.ds(block, 1), :] = merged[block][G : G + 1]
-        for r in range(0, rows, step_rows):
-            rr = pl.ds(pl.multiple_of(block * rows + r, step_rows), step_rows)
-            t = table[r : r + step_rows]
-            g = g_all[rr, :]
-            off = jnp.broadcast_to(t[:, G - 1 : G], g.shape)
+    chunk = min(LANES, half)
+
+    def slope(chip, start, size):
+        qq = span(chip, pair)
+        table = jnp.concatenate([merged[2 * chip], merged[2 * chip + 1]], axis=1)
+        w = w_ref[pl.ds(chip, 1), :]
+        loss_ref[pl.ds(chip, 1), :] = table[G : G + 1]
+
+        def body(j, carry):
+            cc = pl.ds(pl.multiple_of(start + j * chunk, chunk), chunk)
+            g = g_all[cc, qq]
+            off = jnp.broadcast_to(table[G - 1 : G], g.shape)
             for b in range(G - 2, -1, -1):
-                off = jnp.where(g <= b, t[:, b : b + 1], off)
-            w = t[:, G + 1 : G + 2]
-            slopes[rr, :] = (w * jnp.exp2(s_all[rr, :] + off) - w).astype(BF16)
+                off = jnp.where(g <= b, table[b : b + 1], off)
+            slopes[cc, qq] = (w * jnp.exp2(s_all[cc, qq] + off) - w).astype(BF16)
+            return carry
+
+        if size == chunk:
+            body(0, 0)
+        else:
+            lax.fori_loop(0, size // chunk, body, 0)
 
     def k_copy(chip):
         return remote(
@@ -384,7 +396,9 @@
     def q_grad(t):
         out, dm = at.item(t)
         chip = at.chip(out, dm)
-        part = jnp.dot(slopes[span(chip, pair), :], c_all[...], preferred_element_type=F32) * scaling
+        part = lax.dot_general(
+            slopes[:, span(chip, pair)], c_all[...], (((0,), (0,)), ((), ())), preferred_element_type=F32
+        ) * scaling
         q_part[chip] = part.astype(BF16).reshape(2, rows, width)
         k_copy(chip).start()
 
@@ -444,7 +458,6 @@
             z_part[out, sub_rows(s)] = acc[...].astype(BF16)
             z_copy(out, s).start()
 
-    chunk = min(LANES, half)
     per = half // chunk
     n_x = per * (n_pb - 1)
 
@@ -457,20 +470,21 @@
         )
 
     def c_grad(start):
-        return lax.dot_general(
-            slopes[:, pl.ds(pl.multiple_of(start, chunk), chunk)], q_all[...],
-            (((0,), (0,)), ((), ())), preferred_element_type=F32,
-        ) * scaling
+        here = slopes[pl.ds(pl.multiple_of(start, chunk), chunk), :]
+        return jnp.dot(here, q_all[...], preferred_element_type=F32) * scaling
 
     def c_far(r):
         other = lax.rem(at.p + 1 + r // per, n_pb)
         c_part[r] = c_grad(other * half + lax.rem(r, per) * chunk).astype(BF16)
         x_copy(r).start()
 
+    def slope_first(i, carry):
+        slope(i, lax.rem(at.p + 1, n_pb) * half, chunk)
+        return carry
+
     def slope_step(i, carry):
         out, dm = at.item(i)
-        for c in range(2):
-            slope(at.chip(out, dm) * 2 + c)
+        slope(at.chip(out, dm), 0, cols)
 
         @pl.when(i == 0)
         def _():
@@ -482,10 +496,12 @@
 
         return carry
 
+    lax.fori_loop(0, chips, slope_first, 0)
+    c_far(0)
     lax.fori_loop(0, chips, slope_step, 0)
 
     def grad_step(j, carry):
-        @pl.when(j < n_x)
+        @pl.when((j > 0) & (j < n_x))
         def _():
             c_far(j)
 
@@ -558,8 +574,8 @@
         return carry
 
     lax.fori_loop(0, outs, drain, 0)
-    for d, s in far_parts:
-        c_copy(d, s).wait_send()
+    for r in range(n_far):
+        c_copy(r).wait_send()
     for o in others:
         stat_copy(o).wait_send()
         merged_copy(o).wait_send()
@@ -572,7 +588,7 @@
     half = candidates.shape[0]
     tall, cols = grades.shape
     scaling = 1.0 / math.sqrt(width)
-    pieces = 2 if half % 256 == 0 else 1
+    n_far = len(far_parts_of(half, n_pb))
     outs, chips = n_col // 4, n_col // 2
     chunk = min(LANES, half)
     n_x = half // chunk * (n_pb - 1)
@@ -581,9 +597,9 @@
     vmem = pl.BlockSpec(memory_space=pltpu.VMEM)
     hbm = pl.BlockSpec(memory_space=pl.ANY)
     losses, query_grad, cand_grad = pl.pallas_call(
-        functools.partial(kernel, n_col, n_pb, pieces, scaling, cols * n_col),
+        functools.partial(kernel, n_col, n_pb, scaling, cols * n_col),
         out_shape=(
-            jax.ShapeDtypeStruct((n_col, rows), F32),
+            jax.ShapeDtypeStruct((chips, 2 * rows), F32),
             jax.ShapeDtypeStruct((rows, width), BF16),
             jax.ShapeDtypeStruct((half, width), BF16),
         ),
@@ -593,10 +609,11 @@
             pltpu.VMEM((tall, width), BF16),
             pltpu.VMEM((cols, width), BF16),
             pltpu.VMEM((tall, cols), jnp.int32),
-            pltpu.VMEM((tall, cols), F32),
-            pltpu.VMEM((tall, cols), BF16),
-            pltpu.VMEM((n_col, 1 + pieces * (n_pb - 1), STATS, rows), F32),
-            pltpu.VMEM((n_col, 8, rows), F32),
+            pltpu.VMEM((cols, tall), jnp.int32),
+            pltpu.VMEM((cols, tall), F32),
+            pltpu.VMEM((cols, tall), BF16),
+            pltpu.VMEM((chips, 1 + n_far, STATS, 2 * rows), F32),
+            pltpu.VMEM((8, tall), F32),
             pltpu.VMEM((n_col, STATS, rows), F32),
             pltpu.VMEM((n_col, STATS, rows), F32),
             pltpu.VMEM((8, rows), F32),
@@ -611,11 +628,11 @@
             pltpu.VMEM((half, width), F32),
             pltpu.VMEM((n_pb - 1, half, width), BF16),
             dma((2,)),
-            dma((chips,)),
+            dma((tall // (8 * LANES),)),
             dma((n_col, 4, SUBS)),
             dma((n_col, SUBS)),
-            dma((n_pb, pieces)),
-            dma((n_pb, pieces)),
+            dma((n_far,)),
+            dma((n_far,)),
             dma((n_col,)),
             dma((n_col,)),
             dma((n_col,)),
@@ -633,7 +650,7 @@
             collective_id=0, has_side_effects=True, vmem_limit_bytes=62 * 2**20
         ),
         name="listmle",
-    )(queries, candidates, grades, query_weights.reshape(n_col, rows))
+    )(queries, candidates, grades, query_weights.reshape(chips, 2 * rows))
     return (losses.reshape(-1), query_grad, cand_grad)
 
 

time: 102 us -> 102 us (level)
  local copies, waits for them, and re-layouts: 5.23 us -> 6.53 us
    reshape x0 -> x1, local copies, waits for them, and re-layouts: none -> 1.3 us  [local(): query_weights.reshape(chips, 2 * rows)]
where the time goes in v2:
time: 102 us; the launch traced here: 101 us
  Pallas kernels  94.2 us (92%)
  local copies, waits for them, and re-layouts  6.53 us (6%)
    pallas_call x1, Pallas kernels, local(): pl.pallas_call(functools.partial(kernel, n_col, n_pb, scaling, cols * n_c...  94.2 us
    unnamed x3, local copies, waits for them, and re-layouts  5.23 us

profile of v2, /device:TPU:24, one launch (start us, length us, event | category | flops | bytes accessed | tf_op | source)
XLA Modules:
  0.0 101.3 jit_solution(7255316860657931038)
XLA Ops:
  0.6 1.3 %reshape.12.w_ref = f32[8,256]{1,0:T(8,128)} reshape(f32[2048]{0:T(1024)} %param.7) | data formatting | bytes 16384 | tf_op jit(solution)/shard_map/reshape | solution.py:653
  1.9 94.2 %listmle.1 = (f32[8,256]{1,0:T(8,128)}, bf16[128,1024]{1,0:T(8,128)(2,1)}, bf16[512,1024]{1,0:T(8,128)(2,1)}) custom-call(bf16[128,1024]{1,0:T(8,128)(2,1)} %q_hbm.1, bf16[512,1024]{1,0:T(8,128)(2,1)} %c_hbm.1, s32[2048,1024]{1,0:T(8,128)} %g_hbm.1, f32[8,256]{1,0:T(8,128)} %reshape.12.w_ref), custom_call_target="tpu_custom_call" | custom-call | tf_op jit(solution)/shard_map/listmle/pallas_call | solution.py:599
  96.1 1.3 %copy.7 = f32[1,2,8,128]{3,1,2,0:T(2,128)} copy(f32[1,2,8,128]{3,2,1,0:T(8,128)} %bitcast.3) | data formatting | bytes 16384
  97.4 1.7 %copy.10 = bf16[128,1024]{1,0:T(8,128)(2,1)} copy(bf16[128,1024]{1,0:T(8,128)(2,1)} %get-tuple-element.13) | data formatting | bytes 524288
  99.1 2.3 %copy.11 = bf16[512,1024]{1,0:T(8,128)(2,1)} copy(bf16[512,1024]{1,0:T(8,128)(2,1)} %get-tuple-element.14) | data formatting | bytes 2097152

commit v3 on v2

--- a/solution.py
+++ b/solution.py
@@ -10,6 +10,7 @@
 
 GRADES = 5
 STATS = 16
+COUNT_ROWS = (5, 6, 7, 14)
 LOWEST = -1e30
 LANES = 128
 SUBS = 2
@@ -76,25 +77,30 @@
     e = jnp.exp2(s - picked)
     sums = [jnp.sum(jnp.where(g <= b, e, 0.0), axis=0, keepdims=True) for b in range(GRADES - 1)]
     sums.append(jnp.sum(e, axis=0, keepdims=True))
-    for i, row in enumerate(tops + sums + [jnp.sum(s, axis=0, keepdims=True)]):
-        put(i, row)
+    for b in range(GRADES):
+        put(b, tops[b])
+        put(8 + b, sums[b] - sums[b - 1] if b else sums[b])
+    put(8 + GRADES, jnp.sum(s, axis=0, keepdims=True))
 
 
 def finish(got, n_col, cols, columns):
     G = GRADES
-    tops = got[0][:G]
+    rows = got.shape[2]
+    graded = lax.broadcasted_iota(jnp.int32, (8, rows), 0) < G
+    tops = got[0][:8]
+    first = jnp.zeros_like(tops)
     for k in range(1, n_col):
-        tops = jnp.maximum(tops, got[k][:G])
-    masses = jnp.zeros_like(tops)
-    rest = jnp.zeros((STATS - 2 * G, tops.shape[1]), F32)
+        tops = jnp.maximum(tops, got[k][:8])
+    second = first
     for k in range(n_col):
         block = got[k]
-        masses = masses + block[G : 2 * G] * jnp.exp2(block[:G] - tops)
-        rest = rest + block[2 * G :]
+        first = first + block[:8]
+        second = second + block[8:] * jnp.where(graded, jnp.exp2(block[:8] - tops), 1.0)
     top = [tops[b : b + 1] for b in range(G)]
-    mass = [masses[b : b + 1] for b in range(G)]
-    total = rest[:1]
-    count = [rest[b + 1 : b + 2] for b in range(G - 1)]
+    mass = [second[b : b + 1] for b in range(G)]
+    total = second[G : G + 1]
+    both = jnp.concatenate([first, second], axis=0)
+    count = [both[r : r + 1] for r in COUNT_ROWS]
     count.append(float(cols * n_col) - (count[0] + count[1] + count[2] + count[3]))
     levels = []
     seen = jnp.zeros_like(total)
@@ -172,10 +178,10 @@
         ref = q_all.at[q_span(block, s)]
         return remote(ref, ref, q_send.at[block, t, s], q_recv.at[block, s], at.dev(col))
 
-    def forward(k, dm, act):
+    def forward(k, dm, act, subs=range(SUBS)):
         out = at.visit(k)
         block = at.block(out, dm, 0)
-        for s in range(SUBS):
+        for s in subs:
             if act and not (isinstance(k, int) and k == 0 and dm == 0):
                 q_copy(block, s, 0, at.me).wait_recv()
 
@@ -214,6 +220,14 @@
 
     own_q.wait()
     forward(0, 0, True)
+    counts[...] = jnp.zeros(counts.shape, F32)
+
+    def clear(chip, carry):
+        for h in range(n_far + 1):
+            tables[chip, h] = jnp.zeros((STATS, pair), F32)
+        return carry
+
+    lax.fori_loop(0, chips, clear, 0)
     own_c.wait()
     for r in range(n_far):
         c_copy(r).start()
@@ -245,7 +259,8 @@
         for i in range(8):
             for b in range(G - 1):
                 field = (jnp.right_shift(codes[i], 8 * b) & 255).astype(F32)
-                counts[b : b + 1, h + i * LANES : h + (i + 1) * LANES] = jnp.sum(field, axis=0, keepdims=True)
+                row = COUNT_ROWS[b]
+                counts[row : row + 1, h + i * LANES : h + (i + 1) * LANES] = jnp.sum(field, axis=0, keepdims=True)
 
     def score(chip, wide, start, size, part):
         cc = pl.ds(pl.multiple_of(start, size), size)
@@ -266,48 +281,49 @@
     def near(k, dm):
         score(at.chip(at.visit(k), dm), pair, at.p * half, half, 0)
 
-    def far(k, r):
+    def far(k, r, dm=None):
         d, first, n = parts[r]
-        score(2 * at.visit(k), quad, lax.rem(at.p + n_pb - d, n_pb) * half + first, n, r + 1)
+        chip, wide = (2 * at.visit(k), quad) if dm is None else (at.chip(at.visit(k), dm), pair)
+        score(chip, wide, lax.rem(at.p + n_pb - d, n_pb) * half + first, n, r + 1)
 
     def stat_copy(block):
         return remote(stats.at[block], got.at[at.me], s_send.at[block], s_recv.at[at.me], at.dev(block))
 
-    def join(k):
-        for m in range(2):
-            chip = 2 * at.visit(k) + m
+    def join(ks):
+        todo = [2 * at.visit(k) + m for k in ks for m in range(2)]
+        for chip in todo:
             tabs = [tables[chip, h] for h in range(n_far + 1)]
-            top = tabs[0][:G]
+            top = tabs[0][:8]
             for tab in tabs[1:]:
-                top = jnp.maximum(top, tab[:G])
-            mass = jnp.zeros_like(top)
-            total = jnp.zeros((1, pair), F32)
-            for tab in tabs:
-                upto = tab[G : 2 * G]
-                own = jnp.concatenate([upto[:1], upto[1:] - upto[:-1]], axis=0)
-                mass = mass + own * jnp.exp2(tab[:G] - top)
-                total = total + tab[2 * G : 2 * G + 1]
-            count = counts[:, span(chip, pair)][: G - 1]
-            whole = jnp.concatenate([top, mass, total, count, jnp.zeros((1, pair), F32)], axis=0)
+                top = jnp.maximum(top, tab[:8])
+            mass = sum(tab[8:] * jnp.exp2(tab[:8] - top) for tab in tabs)
+            count = counts[:, span(chip, pair)]
             for c in range(2):
-                block = chip * 2 + c
-                stats[block] = whole[:, c * rows : (c + 1) * rows]
-
-                @pl.when(block != at.me)
+                here = slice(c * rows, (c + 1) * rows)
+                stats[chip * 2 + c, :8] = (top + count[:8])[:, here]
+                stats[chip * 2 + c, 8:] = (mass + count[8:])[:, here]
+        for chip in todo:
+            for c in range(2):
+                @pl.when(chip * 2 + c != at.me)
                 def _():
-                    stat_copy(block).start()
+                    stat_copy(chip * 2 + c).start()
 
     partner(0, 0)
+    near(0, 0)
+    if outs > 1:
+        forward(1, 0, True, [0])
 
     def step(u, carry):
-        @pl.when(u > 0)
-        def _():
-            forward(u, 0, True)
-            forward(u - 1, 1, True)
-            partner(u - 1, 1)
-            near(u - 1, 1)
-            partner(u, 0)
-
+        forward(u, 0, True, range(1, SUBS))
+        forward(u - 1, 1, True)
+        partner(u - 1, 1)
+        near(u - 1, 1)
+
+        @pl.when(u + 1 < outs)
+        def _():
+            forward(u + 1, 0, True, [0])
+
+        partner(u, 0)
         near(u, 0)
 
         @pl.when(u == 2)
@@ -322,33 +338,32 @@
 
         return carry
 
-    lax.fori_loop(0, outs, step, 0)
+    lax.fori_loop(1, outs, step, 0)
     if outs < 3:
         for r in range(early):
             c_arrived(r)
     for k in range(max(outs - 2, 0), outs - 1):
         for r in range(early):
             far(k, r)
-    for r in range(early, n_far):
-        c_arrived(r)
-
-        def body(k, carry, r=r):
-            far(k, r)
-            return carry
-
-        lax.fori_loop(0, outs - 1, body, 0)
-
-    def joins(k, carry):
-        join(k)
-        return carry
-
-    lax.fori_loop(0, outs - 1, joins, 0)
+    for r in range(n_far):
+        if r >= early:
+            c_arrived(r)
+
+            def body(k, carry, r=r):
+                far(k, r)
+                return carry
+
+            lax.fori_loop(0, outs - 1, body, 0)
+        far(outs - 1, r, 0)
+
     forward(outs - 1, 1, True)
+
+    join(range(outs - 1))
     partner(outs - 1, 1)
     near(outs - 1, 1)
     for r in range(n_far):
-        far(outs - 1, r)
-    join(outs - 1)
+        far(outs - 1, r, 1)
+    join([outs - 1])
 
     others = [lax.rem(at.me + d, n_col) for d in range(1, n_col)]
     got[at.me] = stats[at.me]
@@ -370,8 +385,11 @@
     def slope(chip, start, size):
         qq = span(chip, pair)
         table = jnp.concatenate([merged[2 * chip], merged[2 * chip + 1]], axis=1)
-        w = w_ref[pl.ds(chip, 1), :]
-        loss_ref[pl.ds(chip, 1), :] = table[G : G + 1]
+        few = pair // LANES
+        w = [w_ref[pl.ds(chip * few + x, 1), :] for x in range(few)]
+        w = jnp.concatenate(w, axis=1)
+        for x in range(0, pair, LANES):
+            loss_ref[pl.ds(chip * (pair // LANES) + x // LANES, 1), :] = table[G : G + 1, x : x + LANES]
 
         def body(j, carry):
             cc = pl.ds(pl.multiple_of(start + j * chunk, chunk), chunk)
@@ -500,6 +518,8 @@
     c_far(0)
     lax.fori_loop(0, chips, slope_step, 0)
 
+    edge = (at.out == 0) | (at.out == outs - 1)
+
     def grad_step(j, carry):
         @pl.when((j > 0) & (j < n_x))
         def _():
@@ -513,6 +533,10 @@
         def _():
             cross(at.item(j)[0])
 
+        @pl.when((j == 2) & edge)
+        def _():
+            chain(outs - 1)
+
         return carry
 
     lax.fori_loop(0, max(n_x, chips - 1), grad_step, 0)
@@ -522,9 +546,11 @@
         return carry
 
     def chain_step(i, carry):
-        chain(outs - 1 - i)
-
-        @pl.when(i == 0)
+        @pl.when((i > 0) | jnp.logical_not(edge))
+        def _():
+            chain(outs - 1 - i)
+
+        @pl.when(i == min(1, outs - 2))
         def _():
             lax.fori_loop(0, per, c_near, 0)
 
@@ -580,6 +606,34 @@
         stat_copy(o).wait_send()
         merged_copy(o).wait_send()
     lax.fori_loop(0, n_x, lambda r, c: (x_copy(r).wait_send(), c)[1], 0)
+
+
+def copy_kernel(*refs):
+    n = (len(refs) - 2) // 3
+    sources, outs, held = refs[:n], refs[n : 2 * n], refs[2 * n : 3 * n]
+    into, back = refs[3 * n :]
+    reads = [pltpu.make_async_copy(a, h, into.at[i]) for i, (a, h) in enumerate(zip(sources, held))]
+    writes = [pltpu.make_async_copy(h, o, back.at[i]) for i, (h, o) in enumerate(zip(held, outs))]
+    for read in reads:
+        read.start()
+    for read, write in zip(reads, writes):
+        read.wait()
+        write.start()
+    for write in writes:
+        write.wait()
+
+
+def settle(arrays):
+    hbm = pl.BlockSpec(memory_space=pl.ANY)
+    dma = pltpu.SemaphoreType.DMA((len(arrays),))
+    return pl.pallas_call(
+        copy_kernel,
+        out_shape=tuple(jax.ShapeDtypeStruct(a.shape, a.dtype) for a in arrays),
+        in_specs=[hbm] * len(arrays),
+        out_specs=(hbm,) * len(arrays),
+        scratch_shapes=[pltpu.VMEM(a.shape, a.dtype) for a in arrays] + [dma, dma],
+        name="settle",
+    )(*arrays)
 
 
 def local(queries, candidates, grades, query_weights):
@@ -596,10 +650,10 @@
     dma = pltpu.SemaphoreType.DMA
     vmem = pl.BlockSpec(memory_space=pltpu.VMEM)
     hbm = pl.BlockSpec(memory_space=pl.ANY)
-    losses, query_grad, cand_grad = pl.pallas_call(
+    outputs = pl.pallas_call(
         functools.partial(kernel, n_col, n_pb, scaling, cols * n_col),
         out_shape=(
-            jax.ShapeDtypeStruct((chips, 2 * rows), F32),
+            jax.ShapeDtypeStruct((tall // LANES, LANES), F32),
             jax.ShapeDtypeStruct((rows, width), BF16),
             jax.ShapeDtypeStruct((half, width), BF16),
         ),
@@ -613,7 +667,7 @@
             pltpu.VMEM((cols, tall), F32),
             pltpu.VMEM((cols, tall), BF16),
             pltpu.VMEM((chips, 1 + n_far, STATS, 2 * rows), F32),
-            pltpu.VMEM((8, tall), F32),
+            pltpu.VMEM((STATS, tall), F32),
             pltpu.VMEM((n_col, STATS, rows), F32),
             pltpu.VMEM((n_col, STATS, rows), F32),
             pltpu.VMEM((8, rows), F32),
@@ -650,7 +704,8 @@
             collective_id=0, has_side_effects=True, vmem_limit_bytes=62 * 2**20
         ),
         name="listmle",
-    )(queries, candidates, grades, query_weights.reshape(chips, 2 * rows))
+    )(queries, candidates, grades, query_weights.reshape(tall // LANES, LANES))
+    losses, cand_grad, query_grad = settle((outputs[0], outputs[2], outputs[1]))
     return (losses.reshape(-1), query_grad, cand_grad)
 
 

time: 102 us -> 96.3 us (0.944)
  local copies, waits for them, and re-layouts: 6.53 us -> 0 us
  Pallas kernels: 94.2 us -> 95.3 us
    unnamed x3 -> x0, local copies, waits for them, and re-layouts: 5.23 us -> none
    pallas_call x0 -> x1, Pallas kernels: none -> 2.34 us  [settle(): pl.pallas_call(copy_kernel, out_shape=tuple((jax.ShapeDtypeStruct(a.shape...]
    reshape x1 -> x0, local copies, waits for them, and re-layouts: 1.3 us -> none  [local(): query_weights.reshape(chips, 2 * rows)]
    pallas_call x1, Pallas kernels: 94.2 us -> 92.9 us  [local(): pl.pallas_call(functools.partial(kernel, n_col, n_pb, scaling, cols * n_c...]
where the time goes in v3:
time: 96.3 us; the launch traced here: 96.1 us
  Pallas kernels  95.3 us (99%)
    pallas_call x1, Pallas kernels, local(): pl.pallas_call(functools.partial(kernel, n_col, n_pb, scaling, cols * n_c...  92.9 us
    pallas_call x1, Pallas kernels, settle(): pl.pallas_call(copy_kernel, out_shape=tuple((jax.ShapeDtypeStruct(a.shape...  2.34 us

profile of v3, /device:TPU:24, one launch (start us, length us, event | category | flops | bytes accessed | tf_op | source)
XLA Modules:
  0.0 96.1 jit_solution(18268171797667910111)
XLA Ops:
  0.6 92.9 %listmle.1 = (f32[16,128]{1,0:T(8,128)}, bf16[128,1024]{1,0:T(8,128)(2,1)}, bf16[512,1024]{1,0:T(8,128)(2,1)}) custom-call(bf16[128,1024]{1,0:T(8,128)(2,1)} %q_hbm.1, bf16[512,1024]{1,0:T(8,128)(2,1)} %c_hbm.1, s32[2048,1024]{1,0:T(8,128)} %g_hbm.1, f32[16,128]{1,0:T(8,128)} %bitcast.2), custom_call_target="tpu_custom_call" | custom-call | tf_op jit(solution)/shard_map/listmle/pallas_call | solution.py:653
  93.6 2.3 %settle.1 = (f32[16,128]{1,0:T(8,128)}, bf16[512,1024]{1,0:T(8,128)(2,1)}, bf16[128,1024]{1,0:T(8,128)(2,1)}) custom-call(f32[16,128]{1,0:T(8,128)} %get-tuple-element.9.refs_0_, bf16[512,1024]{1,0:T(8,128)(2,1)} %get-tuple-element.10.refs_1_, bf16[128,1024]{1,0:T(8,128)(2,1)} %get-tuple-element.11.refs_2_), custom_call_target="tpu_custom_call" | custom-call | tf_op jit(solution)/shard_map/settle/pallas_call | solution.py:629

commit v4 on v3

--- a/solution.py
+++ b/solution.py
@@ -145,6 +145,7 @@
     sub = rows // SUBS
     outs, chips = at.outs, at.chips
     G = GRADES
+    chunk = min(LANES, half)
     parts = far_parts_of(half, n_pb)
     n_far = len(parts)
     early = n_pb - 1
@@ -212,10 +213,13 @@
         other = lax.rem(at.p + d, n_pb)
         return remote(ref, ref, c_send.at[r], c_recv.at[r], {"pb": other, "col": at.me})
 
+    def c_first(r):
+        d, first, n = parts[r]
+        return lax.rem(at.p + n_pb - d, n_pb) * half + first
+
     def c_arrived(r):
-        d, first, n = parts[r]
-        other = lax.rem(at.p + n_pb - d, n_pb)
-        ref = c_all.at[pl.ds(pl.multiple_of(other * half + first, n), n)]
+        n = parts[r][2]
+        ref = c_all.at[pl.ds(pl.multiple_of(c_first(r), n), n)]
         remote(ref, ref, c_send.at[r], c_recv.at[r], at.dev(at.me)).wait_recv()
 
     own_q.wait()
@@ -282,9 +286,11 @@
         score(at.chip(at.visit(k), dm), pair, at.p * half, half, 0)
 
     def far(k, r, dm=None):
-        d, first, n = parts[r]
         chip, wide = (2 * at.visit(k), quad) if dm is None else (at.chip(at.visit(k), dm), pair)
-        score(chip, wide, lax.rem(at.p + n_pb - d, n_pb) * half + first, n, r + 1)
+        score(chip, wide, c_first(r), parts[r][2], r + 1)
+
+    def each(last, task):
+        lax.fori_loop(0, last, lambda j, c: (task(j), c)[1], 0)
 
     def stat_copy(block):
         return remote(stats.at[block], got.at[at.me], s_send.at[block], s_recv.at[at.me], at.dev(block))
@@ -348,12 +354,7 @@
     for r in range(n_far):
         if r >= early:
             c_arrived(r)
-
-            def body(k, carry, r=r):
-                far(k, r)
-                return carry
-
-            lax.fori_loop(0, outs - 1, body, 0)
+            each(outs - 1, lambda k, r=r: far(k, r))
         far(outs - 1, r, 0)
 
     forward(outs - 1, 1, True)
@@ -379,8 +380,6 @@
     merged[at.me] = mine[...]
     for o in others:
         remote(mine, merged.at[o], m_send.at[o], m_recv.at[o], at.dev(at.me)).wait_recv()
-
-    chunk = min(LANES, half)
 
     def slope(chip, start, size):
         qq = span(chip, pair)
@@ -550,7 +549,7 @@
         def _():
             chain(outs - 1 - i)
 
-        @pl.when(i == min(1, outs - 2))
+        @pl.when((i == 0) & jnp.logical_not(edge) | (i == min(1, outs - 2)) & edge)
         def _():
             lax.fori_loop(0, per, c_near, 0)
 

time: 96.3 us -> 93.4 us (0.970)
  Pallas kernels: 95.3 us -> 92.4 us
    pallas_call x1, Pallas kernels: 92.9 us -> 90 us  [local(): pl.pallas_call(functools.partial(kernel, n_col, n_pb, scaling, cols * n_c...]
where the time goes in v4:
time: 93.4 us; the launch traced here: 93.2 us
  Pallas kernels  92.4 us (99%)
    pallas_call x1, Pallas kernels, local(): pl.pallas_call(functools.partial(kernel, n_col, n_pb, scaling, cols * n_c...  90 us
    pallas_call x1, Pallas kernels, settle(): pl.pallas_call(copy_kernel, out_shape=tuple((jax.ShapeDtypeStruct(a.shape...  2.34 us

profile of v4, /device:TPU:24, one launch (start us, length us, event | category | flops | bytes accessed | tf_op | source)
XLA Modules:
  0.0 93.2 jit_solution(2677446217790035190)
XLA Ops:
  0.6 90.0 %listmle.1 = (f32[16,128]{1,0:T(8,128)}, bf16[128,1024]{1,0:T(8,128)(2,1)}, bf16[512,1024]{1,0:T(8,128)(2,1)}) custom-call(bf16[128,1024]{1,0:T(8,128)(2,1)} %q_hbm.1, bf16[512,1024]{1,0:T(8,128)(2,1)} %c_hbm.1, s32[2048,1024]{1,0:T(8,128)} %g_hbm.1, f32[16,128]{1,0:T(8,128)} %bitcast.2), custom_call_target="tpu_custom_call" | custom-call | tf_op jit(solution)/shard_map/listmle/pallas_call | solution.py:652
  90.7 2.3 %settle.1 = (f32[16,128]{1,0:T(8,128)}, bf16[512,1024]{1,0:T(8,128)(2,1)}, bf16[128,1024]{1,0:T(8,128)(2,1)}) custom-call(f32[16,128]{1,0:T(8,128)} %get-tuple-element.9.refs_0_, bf16[512,1024]{1,0:T(8,128)(2,1)} %get-tuple-element.10.refs_1_, bf16[128,1024]{1,0:T(8,128)(2,1)} %get-tuple-element.11.refs_2_), custom_call_target="tpu_custom_call" | custom-call | tf_op jit(solution)/shard_map/settle/pallas_call | solution.py:628

commit v5 on v4

--- a/solution.py
+++ b/solution.py
@@ -131,10 +131,10 @@
 
 def kernel(
     n_col, n_pb, scaling, columns,
-    q_hbm, c_hbm, g_hbm, w_ref, loss_ref, q_out, c_out,
+    q_hbm, c_hbm, g_hbm, w_ref, loss_hbm, q_end, c_end, loss_ref, q_out, c_out,
     q_all, c_all, g_raw, g_all, s_all, slopes, tables, counts, stats, got, mine, merged,
     q_part, core_got, y_got, z_got, z_part, acc, c_part, c_own, c_got,
-    own_sem, g_sem, q_send, q_recv, c_send, c_recv, s_send, s_recv, m_send, m_recv,
+    out_sem, own_sem, g_sem, q_send, q_recv, c_send, c_recv, s_send, s_recv, m_send, m_recv,
     k_send, k_recv, y_send, y_recv, z_send, z_recv, x_send, x_recv,
 ):
     at = Place(n_col, n_pb)
@@ -285,9 +285,8 @@
     def near(k, dm):
         score(at.chip(at.visit(k), dm), pair, at.p * half, half, 0)
 
-    def far(k, r, dm=None):
-        chip, wide = (2 * at.visit(k), quad) if dm is None else (at.chip(at.visit(k), dm), pair)
-        score(chip, wide, c_first(r), parts[r][2], r + 1)
+    def far(k, r):
+        score(2 * at.visit(k), quad, c_first(r), parts[r][2], r + 1)
 
     def each(last, task):
         lax.fori_loop(0, last, lambda j, c: (task(j), c)[1], 0)
@@ -351,19 +350,18 @@
     for k in range(max(outs - 2, 0), outs - 1):
         for r in range(early):
             far(k, r)
-    for r in range(n_far):
-        if r >= early:
-            c_arrived(r)
-            each(outs - 1, lambda k, r=r: far(k, r))
-        far(outs - 1, r, 0)
-
-    forward(outs - 1, 1, True)
-
+    for r in range(early, n_far):
+        if r == n_far - early:
+            forward(outs - 1, 1, True)
+        c_arrived(r)
+        each(outs - 1, lambda k, r=r: far(k, r))
+    if n_far == early:
+        forward(outs - 1, 1, True)
     join(range(outs - 1))
     partner(outs - 1, 1)
     near(outs - 1, 1)
     for r in range(n_far):
-        far(outs - 1, r, 1)
+        far(outs - 1, r)
     join([outs - 1])
 
     others = [lax.rem(at.me + d, n_col) for d in range(1, n_col)]
@@ -570,6 +568,15 @@
 
         q_out[sub_rows(s), :] = acc[...].astype(BF16)
 
+    loss_copy = pltpu.make_async_copy(loss_ref, loss_hbm, out_sem.at[0])
+    q_end_copy = pltpu.make_async_copy(q_out, q_end, out_sem.at[1])
+    loss_copy.start()
+    q_end_copy.start()
+
+    def c_end_copy(j):
+        rr = pl.ds(pl.multiple_of(j * chunk, chunk), chunk)
+        return pltpu.make_async_copy(c_out.at[rr], c_end.at[rr], out_sem.at[2 + j])
+
     def c_finish(j, carry):
         rr = pl.ds(pl.multiple_of(j * chunk, chunk), chunk)
         total = c_own[rr]
@@ -579,6 +586,7 @@
             remote(ref, ref, x_send.at[r], x_recv.at[r], at.dev(at.me)).wait_recv()
             total = total + c_got[d - 1, rr].astype(F32)
         c_out[rr] = total.astype(BF16)
+        c_end_copy(j).start()
         return carry
 
     lax.fori_loop(0, per, c_finish, 0)
@@ -605,6 +613,9 @@
         stat_copy(o).wait_send()
         merged_copy(o).wait_send()
     lax.fori_loop(0, n_x, lambda r, c: (x_copy(r).wait_send(), c)[1], 0)
+    loss_copy.wait()
+    q_end_copy.wait()
+    lax.fori_loop(0, per, lambda j, c: (c_end_copy(j).wait(), c)[1], 0)
 
 
 def copy_kernel(*refs):
@@ -657,8 +668,11 @@
             jax.ShapeDtypeStruct((half, width), BF16),
         ),
         in_specs=[hbm, hbm, hbm, vmem],
-        out_specs=(vmem, vmem, vmem),
+        out_specs=(hbm, hbm, hbm),
         scratch_shapes=[
+            pltpu.VMEM((tall // LANES, LANES), F32),
+            pltpu.VMEM((rows, width), BF16),
+            pltpu.VMEM((half, width), BF16),
             pltpu.VMEM((tall, width), BF16),
             pltpu.VMEM((cols, width), BF16),
             pltpu.VMEM((tall, cols), jnp.int32),
@@ -680,6 +694,7 @@
             pltpu.VMEM((n_x, chunk, width), BF16),
             pltpu.VMEM((half, width), F32),
             pltpu.VMEM((n_pb - 1, half, width), BF16),
+            dma((2 + half // chunk,)),
             dma((2,)),
             dma((tall // (8 * LANES),)),
             dma((n_col, 4, SUBS)),

time: 93.4 us -> 91.5 us (0.980)
  Pallas kernels: 92.4 us -> 90.4 us
    pallas_call x1, Pallas kernels: 90 us -> 88.1 us  [local(): pl.pallas_call(functools.partial(kernel, n_col, n_pb, scaling, cols * n_c...]
where the time goes in v5:
time: 91.5 us; the launch traced here: 91.2 us
  Pallas kernels  90.4 us (99%)
    pallas_call x1, Pallas kernels, local(): pl.pallas_call(functools.partial(kernel, n_col, n_pb, scaling, cols * n_c...  88.1 us
    pallas_call x1, Pallas kernels, settle(): pl.pallas_call(copy_kernel, out_shape=tuple((jax.ShapeDtypeStruct(a.shape...  2.34 us

profile of v5, /device:TPU:24, one launch (start us, length us, event | category | flops | bytes accessed | tf_op | source)
XLA Modules:
  0.0 91.2 jit_solution(12540631651612872143)
XLA Ops:
  0.6 88.1 %listmle.1 = (f32[16,128]{1,0:T(8,128)}, bf16[128,1024]{1,0:T(8,128)(2,1)}, bf16[512,1024]{1,0:T(8,128)(2,1)}) custom-call(bf16[128,1024]{1,0:T(8,128)(2,1)} %q_hbm.1, bf16[512,1024]{1,0:T(8,128)(2,1)} %c_hbm.1, s32[2048,1024]{1,0:T(8,128)} %g_hbm.1, f32[16,128]{1,0:T(8,128)} %bitcast.2), custom_call_target="tpu_custom_call" | custom-call | tf_op jit(solution)/shard_map/listmle/pallas_call | solution.py:663
  88.7 2.3 %settle.1 = (f32[16,128]{1,0:T(8,128)}, bf16[512,1024]{1,0:T(8,128)(2,1)}, bf16[128,1024]{1,0:T(8,128)(2,1)}) custom-call(f32[16,128]{1,0:T(8,128)} %get-tuple-element.9.refs_0_, bf16[512,1024]{1,0:T(8,128)(2,1)} %get-tuple-element.10.refs_1_, bf16[128,1024]{1,0:T(8,128)(2,1)} %get-tuple-element.11.refs_2_), custom_call_target="tpu_custom_call" | custom-call | tf_op jit(solution)/shard_map/settle/pallas_call | solution.py:639

commit v6 on v5

--- a/solution.py
+++ b/solution.py
@@ -71,16 +71,21 @@
 def statistics(s, g, put):
     tops = [jnp.max(jnp.where(g <= b, s, LOWEST), axis=0, keepdims=True) for b in range(GRADES - 1)]
     tops.append(jnp.max(s, axis=0, keepdims=True))
-    picked = jnp.broadcast_to(tops[-1], s.shape)
-    for b in range(GRADES - 2, -1, -1):
-        picked = jnp.where(g <= b, tops[b], picked)
-    e = jnp.exp2(s - picked)
+    e = jnp.exp2(s - pick(jnp.concatenate(tops + [tops[-1]] * (8 - GRADES), axis=0), g))
     sums = [jnp.sum(jnp.where(g <= b, e, 0.0), axis=0, keepdims=True) for b in range(GRADES - 1)]
     sums.append(jnp.sum(e, axis=0, keepdims=True))
     for b in range(GRADES):
         put(b, tops[b])
         put(8 + b, sums[b] - sums[b - 1] if b else sums[b])
     put(8 + GRADES, jnp.sum(s, axis=0, keepdims=True))
+
+
+def pick(table, g):
+    tiles = [
+        [jnp.take_along_axis(table[:, x : x + LANES], g[r : r + 8, x : x + LANES], axis=0) for x in range(0, g.shape[1], LANES)]
+        for r in range(0, g.shape[0], 8)
+    ]
+    return jnp.concatenate([jnp.concatenate(row, axis=1) for row in tiles], axis=0)
 
 
 def finish(got, n_col, cols, columns):
@@ -391,9 +396,7 @@
         def body(j, carry):
             cc = pl.ds(pl.multiple_of(start + j * chunk, chunk), chunk)
             g = g_all[cc, qq]
-            off = jnp.broadcast_to(table[G - 1 : G], g.shape)
-            for b in range(G - 2, -1, -1):
-                off = jnp.where(g <= b, table[b : b + 1], off)
+            off = pick(table, g)
             slopes[cc, qq] = (w * jnp.exp2(s_all[cc, qq] + off) - w).astype(BF16)
             return carry
 

time: 91.5 us -> 90.4 us (0.988)
  Pallas kernels: 90.4 us -> 89.3 us
    pallas_call x1, Pallas kernels: 88.1 us -> 87 us  [local(): pl.pallas_call(functools.partial(kernel, n_col, n_pb, scaling, cols * n_c...]
where the time goes in v6:
time: 90.4 us; the launch traced here: 90.1 us
  Pallas kernels  89.3 us (99%)
    pallas_call x1, Pallas kernels, local(): pl.pallas_call(functools.partial(kernel, n_col, n_pb, scaling, cols * n_c...  87 us
    pallas_call x1, Pallas kernels, settle(): pl.pallas_call(copy_kernel, out_shape=tuple((jax.ShapeDtypeStruct(a.shape...  2.34 us

profile of v6, /device:TPU:24, one launch (start us, length us, event | category | flops | bytes accessed | tf_op | source)
XLA Modules:
  0.0 90.1 jit_solution(4989014717025401168)
XLA Ops:
  0.6 87.0 %listmle.1 = (f32[16,128]{1,0:T(8,128)}, bf16[128,1024]{1,0:T(8,128)(2,1)}, bf16[512,1024]{1,0:T(8,128)(2,1)}) custom-call(bf16[128,1024]{1,0:T(8,128)(2,1)} %q_hbm.1, bf16[512,1024]{1,0:T(8,128)(2,1)} %c_hbm.1, s32[2048,1024]{1,0:T(8,128)} %g_hbm.1, f32[16,128]{1,0:T(8,128)} %bitcast.2), custom_call_target="tpu_custom_call" | custom-call | tf_op jit(solution)/shard_map/listmle/pallas_call | solution.py:666
  87.6 2.3 %settle.1 = (f32[16,128]{1,0:T(8,128)}, bf16[512,1024]{1,0:T(8,128)(2,1)}, bf16[128,1024]{1,0:T(8,128)(2,1)}) custom-call(f32[16,128]{1,0:T(8,128)} %get-tuple-element.9.refs_0_, bf16[512,1024]{1,0:T(8,128)(2,1)} %get-tuple-element.10.refs_1_, bf16[128,1024]{1,0:T(8,128)(2,1)} %get-tuple-element.11.refs_2_), custom_call_target="tpu_custom_call" | custom-call | tf_op jit(solution)/shard_map/settle/pallas_call | solution.py:642
